TPU v7x, 32 devices: a whole 2x2x4 slice. The times are simulated.
32 devices in a mesh: row: 4 (over z), col: 8 (over y, x, core).
Axes of the slice: x: 2, y: 2, z: 4, core: 2. Of those that a mesh axis runs over, the one named last changes fastest.
Arguments:
- diag_blocks: float32 [8, 16, 512, 512], P('row', 'col'), may hold values from -4 to 16, as said below
- horizontal: bfloat16 [8, 16, 512, 512], P('row', 'col'), may hold values from -0.125 to 0.125
- vertical: bfloat16 [8, 16, 512, 512], P('row', 'col'), may hold values from -0.125 to 0.125
Outputs:
- red_factor: float32 [8, 8, 512, 512], P('row', 'col')
- black_schur: float32 [8, 8, 512, 512], P('row', 'col')
- black_links: bfloat16 [8, 8, 4, 512, 512], P('row', 'col')
Inputs may be any that keep to these rules, and one draw needn't show every extreme that they name: `diag_blocks`: every block is symmetric and its eigenvalues are at least 1.
All inputs are finite; a program needn't handle non-finite values.
Results may differ from a plain program's by a relative error of at most 0.0054.
Values may be sent and summed in bfloat16 or wider, within the bound.
A program may use at most 128 MiB of HBM per device.

v0:
```python
import functools

import jax
import jax.numpy as jnp
from jax import lax
from jax.experimental import pallas as pl
from jax.experimental.pallas import tpu as pltpu
from jax.sharding import PartitionSpec as P

PANEL = 128
STRIP = 8
VMEM = pl.BlockSpec(memory_space=pltpu.VMEM)


def split(value):
    high = value.astype(jnp.bfloat16)
    low = (value - high.astype(jnp.float32)).astype(jnp.bfloat16)
    return high, low


def product(left, right):
    dot = functools.partial(jnp.dot, preferred_element_type=jnp.float32)
    (lh, ll), (rh, rl) = left, right
    return dot(lh, rh) + (dot(lh, rl) + dot(ll, rh))


def factor_diagonal(work, count):
    lane = lax.broadcasted_iota(jnp.int32, (STRIP, PANEL), 1)
    sub = lax.broadcasted_iota(jnp.int32, (STRIP, PANEL), 0)
    sub_wide = lax.broadcasted_iota(jnp.int32, (STRIP, 2 * PANEL), 0)

    def strip(b, carry):
        start = pl.multiple_of(b * STRIP, STRIP)
        rows = [work[m, pl.ds(start, STRIP), :] for m in range(count)]
        columns = [
            [
                jnp.take_along_axis(rows[m][:, :PANEL], jnp.full_like(lane, start + c), axis=1)
                for c in range(STRIP)
            ]
            for m in range(count)
        ]
        for j in range(STRIP):
            for m in range(count):
                column = columns[m][j]
                pivot = jnp.broadcast_to(column[j : j + 1], column.shape)
                root = lax.rsqrt(pivot)
                square = root * root
                below = jnp.where(sub > j, column, 0.0)
                for c in range(j + 1, STRIP):
                    across = jnp.broadcast_to(columns[m][c][j : j + 1], column.shape)
                    columns[m][c] = columns[m][c] - (below * across) * square
                row = jnp.broadcast_to(rows[m][j : j + 1], rows[m].shape)
                wide_below = jnp.concatenate([below * square] * 2, 1)
                wide_root = jnp.concatenate([root] * 2, 1)
                rows[m] = jnp.where(sub_wide == j, row * wide_root, rows[m] - wide_below * row)
        for m in range(count):
            work[m, pl.ds(start, STRIP), :] = rows[m]
            high = rows[m].astype(jnp.bfloat16).astype(jnp.float32)
            low = rows[m] - high
            after = lane >= start + STRIP
            left_high = jnp.where(after, high[:, :PANEL], 0.0)
            left_low = jnp.where(after, low[:, :PANEL], 0.0)
            left = jnp.concatenate([left_high, left_high, left_low, left_low], 0)
            right = jnp.concatenate([high, low, high, low], 0)
            work[m] = work[m] - lax.dot_general(
                left.T.astype(jnp.bfloat16),
                right.astype(jnp.bfloat16),
                (((1,), (0,)), ((), ())),
                preferred_element_type=jnp.float32,
            )
        return carry

    lax.fori_loop(0, PANEL // STRIP, strip, 0)


def triangle(order):
    return [(p, q) for p in range(order // PANEL) for q in range(p + 1)]


def factor_kernel(diag, factor, packed, inverse, blocks, work):
    count, order = diag.shape[0], diag.shape[2]
    row = lax.broadcasted_iota(jnp.int32, (PANEL, PANEL), 0)
    col = lax.broadcasted_iota(jnp.int32, (PANEL, PANEL), 1)
    eye = jnp.where(row == col, 1.0, 0.0).astype(jnp.float32)
    for m in range(count):
        blocks[m] = diag[m, m]
    inverse[...] = jnp.zeros_like(inverse)
    factor[...] = jnp.zeros_like(factor)
    for start in range(0, order, PANEL):
        stop = start + PANEL
        here = slice(start, stop)
        for m in range(count):
            work[m, :, :PANEL] = blocks[m, here, here]
            work[m, :, PANEL:] = eye
        factor_diagonal(work, count)
        for m in range(count):
            upper = jnp.where(col >= row, work[m, :, :PANEL], 0.0)
            factor[m, here, here] = upper.T
            small = jnp.where(col <= row, work[m, :, PANEL:], 0.0)
            small_parts = split(small)
            if start:
                inverse[m, here, :start] = product(small_parts, split(inverse[m, here, :start]))
            inverse[m, here, here] = small
            if stop < order:
                across = product(small_parts, split(blocks[m, here, stop:]))
                down = across.T
                factor[m, stop:, here] = down
                down_parts = split(down)
                blocks[m, stop:, stop:] -= product(down_parts, split(across))
                inverse[m, stop:, :stop] -= product(down_parts, split(inverse[m, here, :stop]))


    for m in range(count):
        for n, (p, q) in enumerate(triangle(order)):
            tile = inverse[m, p * PANEL : (p + 1) * PANEL, q * PANEL : (q + 1) * PANEL]
            packed[m, 0, n], packed[m, 1, n] = split(tile)


def factored(diag):
    count, order = diag.shape[0], diag.shape[2]
    whole = (count, order, order)
    packed = (count, 2, len(triangle(order)), PANEL, PANEL)
    return pl.pallas_call(
        factor_kernel,
        out_shape=(
            jax.ShapeDtypeStruct(whole, jnp.float32),
            jax.ShapeDtypeStruct(packed, jnp.bfloat16),
        ),
        in_specs=[VMEM],
        out_specs=(VMEM, VMEM),
        scratch_shapes=[
            pltpu.VMEM(whole, jnp.float32),
            pltpu.VMEM(whole, jnp.float32),
            pltpu.VMEM((count, PANEL, 2 * PANEL), jnp.float32),
        ],
        compiler_params=pltpu.CompilerParams(vmem_limit_bytes=40 * 2**20),
        cost_estimate=pl.CostEstimate(
            flops=20_000_000_000, bytes_accessed=3 * diag.size * 4, transcendentals=0
        ),
    )(diag)


def apply_inverse(packed, m, couplings, full, out):
    order = full.shape[1]
    group = 2 * PANEL
    for p in range(order // PANEL - 1):
        corner = (slice(p * PANEL, (p + 1) * PANEL), slice((p + 1) * PANEL, (p + 2) * PANEL))
        full[0, corner[0], corner[1]] = jnp.zeros((PANEL, PANEL), jnp.bfloat16)
        full[1, corner[0], corner[1]] = jnp.zeros((PANEL, PANEL), jnp.bfloat16)
    for n, (p, q) in enumerate(triangle(order)):
        for part in range(2):
            full[part, p * PANEL : (p + 1) * PANEL, q * PANEL : (q + 1) * PANEL] = packed[m, part, n]
    for start in range(0, order, group):
        stop = start + group
        high, low = full[0, start:stop, :stop], full[1, start:stop, :stop]
        for d, coupling in enumerate(couplings):
            right = coupling[:, :stop] if d < 2 else coupling[:stop, :]
            axes = (((1,), (1 if d < 2 else 0,)), ((), ()))
            dot = functools.partial(
                lax.dot_general, dimension_numbers=axes, preferred_element_type=jnp.float32
            )
            out[d, start:stop, :] = (dot(high, right) + dot(low, right)).astype(jnp.bfloat16)


def own_kernel(packed, edge_left, edge_up, horizontal, vertical, out, full):
    first = (edge_left.at[0, 0], edge_up.at[0, 0], horizontal.at[0, 0], vertical.at[0, 0])
    second = (horizontal.at[1, 0], vertical.at[0, 1], horizontal.at[1, 1], vertical.at[1, 1])
    apply_inverse(packed, 0, first, full, out.at[0, 0])
    apply_inverse(packed, 1, second, full, out.at[1, 0])


def below_kernel(packed, left, up, right, out, full):
    couplings = (left.at[0, 0], up.at[1, 0], right.at[0], right.at[1])
    apply_inverse(packed, 0, couplings, full, out.at[0, 0])


def solved_with(kernel, count, operands):
    order = operands[-1].shape[-1]
    flops = 12 * count * order**3
    return pl.pallas_call(
        kernel,
        out_shape=jax.ShapeDtypeStruct((count, 1, 4, order, order), jnp.bfloat16),
        in_specs=[VMEM] * len(operands),
        out_specs=VMEM,
        scratch_shapes=[pltpu.VMEM((2, order, order), jnp.bfloat16)],
        compiler_params=pltpu.CompilerParams(vmem_limit_bytes=40 * 2**20),
        cost_estimate=pl.CostEstimate(
            flops=flops, bytes_accessed=16 * count * order**2, transcendentals=0
        ),
    )(*operands)


def passed_along(value, axis, by):
    size = lax.axis_size(axis)
    return lax.ppermute(value, axis, [(i, (i + by) % size) for i in range(size)])


def select_colour(blocks, parity):
    grid_rows = blocks.shape[0]
    grid_columns = blocks.shape[1]
    trailing = blocks.shape[2:]
    paired = blocks.reshape((grid_rows // 2, 2, grid_columns // 2, 2) + trailing)
    joined = jnp.stack([paired[:, 0, :, parity], paired[:, 1, :, 1 - parity]], 1)
    return joined.reshape((grid_rows, grid_columns // 2) + trailing)


def combine_rows(even_rows, odd_rows):
    joined = jnp.stack([even_rows, odd_rows], 1)
    return joined.reshape((2 * even_rows.shape[0],) + even_rows.shape[1:])


def gram_term(former, latter):
    return jnp.einsum("rmka,rmkb->rmab", former, latter, preferred_element_type=jnp.float32)


def on_device(diag_blocks, horizontal, vertical):
    edge_up = passed_along(vertical[-1:, :1], "row", 1)
    ahead = passed_along(jnp.stack([horizontal[0, 0], vertical[0, 0]]), "row", -1)
    edge_left = passed_along(horizontal[:1, -1:], "col", 1)
    ahead_left = passed_along(edge_left, "row", -1)
    red_factor, packed = factored(diag_blocks)
    below_packed = passed_along(packed[:1], "row", -1)
    solved = solved_with(own_kernel, 2, (packed, edge_left, edge_up, horizontal, vertical))
    red_factor = red_factor[:, None]
    got_above = passed_along(solved[-1:, :, 3], "row", 1)
    above_down = jnp.concatenate([got_above, solved[:-1, :, 3]], 0)
    got_below = solved_with(below_kernel, 1, (below_packed, ahead_left, vertical, ahead))
    below_all = jnp.concatenate([solved[1:], got_below], 0)
    got_left = passed_along(solved[1::2, -1:, 2:4], "col", 1)
    left_pair = combine_rows(
        solved[0::2, :, 2:4], jnp.concatenate([got_left, solved[1::2, :-1, 2:4]], 1)
    )
    right_first, right_rest = passed_along((solved[0::2, :1, 0], solved[0::2, :1, 2:4]), "col", -1)
    right_left = combine_rows(
        jnp.concatenate([solved[0::2, 1:, 0], right_first], 1), solved[1::2, :, 0]
    )
    right_pair = combine_rows(
        jnp.concatenate([solved[0::2, 1:, 2:4], right_rest], 1), solved[1::2, :, 2:4]
    )
    below_up = below_all[:, :, 1]
    update = gram_term(above_down, above_down) + gram_term(below_up, below_up)
    update = (
        update
        + gram_term(left_pair[:, :, 0], left_pair[:, :, 0])
        + gram_term(right_left, right_left)
    )
    black_schur = select_colour(diag_blocks, 1) - update
    east_link = -gram_term(right_left, right_pair[:, :, 0])
    south_link = -gram_term(below_up, below_all[:, :, 3])
    southeast = -(
        gram_term(right_left, right_pair[:, :, 1]) + gram_term(below_up, below_all[:, :, 2])
    )
    southwest = -(
        gram_term(left_pair[:, :, 0], left_pair[:, :, 1]) + gram_term(below_up, below_all[:, :, 0])
    )
    black_links = jnp.stack([east_link, south_link, southeast, southwest], 2).astype(jnp.bfloat16)
    return (red_factor, black_schur, black_links)


def solution(mesh):
    in_specs = (
        P("row", "col", None, None),
        P("row", "col", None, None),
        P("row", "col", None, None),
    )
    out_specs = (
        P("row", "col", None, None),
        P("row", "col", None, None),
        P("row", "col", None, None, None),
    )
    return jax.shard_map(
        on_device, mesh=mesh, in_specs=in_specs, out_specs=out_specs, check_vma=False
    )
```

profile of v0, /device:TPU:0, one launch (start us, length us, event | category | flops | bytes accessed | tf_op | source)
XLA Modules:
  0.0 96.7 jit_solution(4029797215530310380)
XLA Ops:
  0.6 1.8 %slice_bitcast_fusion.14 = (bf16[1,512,512]{2,1,0:T(8,128)(2,1)S(1)}, bf16[1,1,512,512]{3,2,1,0:T(8,128)(2,1)S(1)}, bf16[1,1,512,512]{3,2,1,0:T(8,128)(2,1)S(1)}, bf16[1,512,512]{2,1,0:T(8,128)(2,1)S(1)}) fusion(bf16[2,2,512,512]{3,2,1,0:T(8,128)(2,1)} %up.1, bf16[2,2,512,512]{3,2,1,0:T(8,128)(2,1)} %horizontal.1), kind=kLoop, calls=%fused_computation.48 | loop fusion | bytes 4194304 | tf_op jit(solution)/shard_map/stack;squeeze | solution.py:218
  3.0 2.6 %collective-permute-start.1 = (bf16[1,1,512,512]{3,2,1,0:T(8,128)(2,1)S(1)}, bf16[1,1,512,512]{3,2,1,0:T(8,128)(2,1)S(1)}, u32[]{:S(2)}, u32[]{:S(2)}) collective-permute-start(bf16[1,1,512,512]{3,2,1,0:T(8,128)(2,1)S(1)} %get-tuple-element.23), channel_id=1, source_target_pairs={{0,8},{8,16},{16,24},{24,0},{1,9},{9,17},{17,25},{25,1},{2,10},{10... | collective-permute-start | bytes 1572872 | tf_op jit(solution)/shard_map/ppermute | solution.py:195
  5.7 2.1 %collective-permute-start.5 = (bf16[2,512,512]{2,1,0:T(8,128)(2,1)S(1)}, bf16[2,512,512]{2,1,0:T(8,128)(2,1)S(1)}, u32[]{:S(2)}, u32[]{:S(2)}) collective-permute-start(bf16[2,512,512]{2,1,0:T(8,128)(2,1)S(1)} %pad_maximum_fusion.2), channel_id=1, source_target_pairs={{0,24},{8,0},{16,8},{24,16},{1,25},{9,1},{17,9},{25,17},{2,26},{10... | collective-permute-start | bytes 3145736 | tf_op jit(solution)/shard_map/ppermute | solution.py:195
  7.9 31.5 %shard_map.58 = (f32[2,512,512]{2,1,0:T(8,128)}, bf16[2,2,10,128,128]{4,3,2,1,0:T(8,128)(2,1)S(1)}) custom-call(f32[2,2,512,512]{3,2,1,0:T(8,128)S(1)} %copy-done.1), custom_call_target="tpu_custom_call" | custom-call | flops 20000000000 | bytes 12582912 | tf_op jit(solution)/shard_map/pallas_call | solution.py:123
  39.4 2.1 %collective-permute-start.3 = (bf16[1,2,10,128,128]{4,3,2,1,0:T(8,128)(2,1)S(1)}, bf16[1,2,10,128,128]{4,3,2,1,0:T(8,128)(2,1)S(1)}, u32[]{:S(2)}, u32[]{:S(2)}) collective-permute-start(bf16[1,2,10,128,128]{4,3,2,1,0:T(8,128)(2,1)S(1)} %slice.81), channel_id=1, source_target_pairs={{0,24},{8,0},{16,8},{24,16},{1,25},{9,1},{17,9},{25,17},{2,26},{10... | collective-permute-start | bytes 1966088 | tf_op jit(solution)/shard_map/ppermute | solution.py:195
  41.5 3.6 %shard_map.59 = bf16[2,1,4,512,512]{4,3,2,1,0:T(8,128)(2,1)S(1)} custom-call(bf16[2,2,10,128,128]{4,3,2,1,0:T(8,128)(2,1)S(1)} %get-tuple-element.6.packed, bf16[1,1,512,512]{3,2,1,0:T(8,128)(2,1)S(1)} %collective-permute-done.edge_left, bf16[1,1,512,512]{3,2,1,0:T(8,128)(2,1)S(1)} %collective-permute-done.1.edge_up, bf16[2,2,512,512]{3,2,1,0:T(8,128)(2,1)S(1)} %copy-done.2, ...), custom_call_target="tpu_custom_call" | custom-call | flops 3221225472 | bytes 8388608 | tf_op jit(solution)/shard_map/pallas_call | solution.py:180
  45.1 1.2 %slice_bitcast_fusion.13 = (bf16[1,1,512,512]{3,2,1,0:T(8,128)(2,1)}, bf16[1,1,1,512,512]{4,3,2,1,0:T(8,128)(2,1)S(1)}, bf16[1,1,512,512]{3,2,1,0:T(8,128)(2,1)}, bf16[1,1,512,512]{3,2,1,0:T(8,128)(2,1)}) fusion(bf16[2,1,4,512,512]{4,3,2,1,0:T(8,128)(2,1)S(1)} %shard_map.59), kind=kLoop, calls=%fused_computation.47 | loop fusion | bytes 4194304 | tf_op jit(solution)/shard_map/squeeze | solution.py:225
  46.3 1.7 %collective-permute-start.7 = (bf16[1,1,512,512]{3,2,1,0:T(8,128)(2,1)}, bf16[1,1,512,512]{3,2,1,0:T(8,128)(2,1)}, u32[]{:S(2)}, u32[]{:S(2)}) collective-permute-start(bf16[1,1,512,512]{3,2,1,0:T(8,128)(2,1)} %get-tuple-element.16), channel_id=1, source_target_pairs={{0,7},{1,0},{2,1},{3,2},{4,3},{5,4},{6,5},{7,6},{8,15},{9,8},{10,9... | collective-permute-start | bytes 1572872 | tf_op jit(solution)/shard_map/ppermute | solution.py:195
  48.8 3.1 %collective-permute-start.8 = (bf16[1,1,2,512,512]{4,3,2,1,0:T(8,128)(2,1)S(1)}, bf16[1,1,2,512,512]{4,3,2,1,0:T(8,128)(2,1)}, u32[]{:S(2)}, u32[]{:S(2)}) collective-permute-start(bf16[1,1,2,512,512]{4,3,2,1,0:T(8,128)(2,1)S(1)} %get-tuple-element.10), channel_id=1, source_target_pairs={{0,7},{1,0},{2,1},{3,2},{4,3},{5,4},{6,5},{7,6},{8,15},{9,8},{10,9... | collective-permute-start | bytes 3145736 | tf_op jit(solution)/shard_map/ppermute | solution.py:195
  52.0 4.8 %collective-permute-done.3.packed = bf16[1,2,10,128,128]{4,3,2,1,0:T(8,128)(2,1)S(1)} collective-permute-done((bf16[1,2,10,128,128]{4,3,2,1,0:T(8,128)(2,1)S(1)}, bf16[1,2,10,128,128]{4,3,2,1,0:T(8,128)(2,1)S(1)}, u32[]{:S(2)}, u32[]{:S(2)}) %collective-permute-start.3) | collective-permute-done | bytes 655392 | tf_op jit(solution)/shard_map/ppermute | solution.py:195
  58.1 10.0 %collective-permute-done.4.left = bf16[1,1,512,512]{3,2,1,0:T(8,128)(2,1)S(1)} collective-permute-done((bf16[1,1,512,512]{3,2,1,0:T(8,128)(2,1)S(1)}, bf16[1,1,512,512]{3,2,1,0:T(8,128)(2,1)S(1)}, u32[]{:S(2)}, u32[]{:S(2)}) %collective-permute-start.4) | collective-permute-done | bytes 524320 | tf_op jit(solution)/shard_map/ppermute | solution.py:195
  68.0 1.8 %shard_map.60 = bf16[1,1,4,512,512]{4,3,2,1,0:T(8,128)(2,1)S(1)} custom-call(bf16[1,2,10,128,128]{4,3,2,1,0:T(8,128)(2,1)S(1)} %collective-permute-done.3.packed, bf16[1,1,512,512]{3,2,1,0:T(8,128)(2,1)S(1)} %collective-permute-done.4.left, bf16[2,2,512,512]{3,2,1,0:T(8,128)(2,1)S(1)} %copy-done, bf16[2,512,512]{2,1,0:T(8,128)(2,1)S(1)} %collective-permute-done.5.right), custom_call_target="tpu_custom_call" | custom-call | flops 1610612736 | bytes 4194304 | tf_op jit(solution)/shard_map/pallas_call | solution.py:180
  69.9 2.0 %fusion.26 = f32[2,512,512]{2,1,0:T(8,128)S(1)} fusion(bf16[1,1,1,512,512]{4,3,2,1,0:T(8,128)(2,1)S(1)} %get-tuple-element.15, bf16[1,1,1,512,512]{4,3,2,1,0:T(8,128)(2,1)} %bitcast.18), kind=kOutput, calls=%fused_computation.50 | convolution fusion | flops 537395200 | bytes 3145728 | tf_op jit(solution)/shard_map/rmka,rmkb->rmab/dot_general | solution.py:213
  71.9 8.1 %collective-permute-done.2 = bf16[1,1,512,512]{3,2,1,0:T(8,128)(2,1)} collective-permute-done((bf16[1,1,512,512]{3,2,1,0:T(8,128)(2,1)}, bf16[1,1,512,512]{3,2,1,0:T(8,128)(2,1)}, u32[]{:S(2)}, u32[]{:S(2)}) %collective-permute-start.2) | collective-permute-done | bytes 524320 | tf_op jit(solution)/shard_map/ppermute | solution.py:195
  80.1 2.0 %fusion.22 = f32[2,512,512]{2,1,0:T(8,128)S(1)} fusion(bf16[1,1,512,512]{3,2,1,0:T(8,128)(2,1)S(1)} %copy-done.5, bf16[1,1,512,512]{3,2,1,0:T(8,128)(2,1)} %collective-permute-done.2), kind=kOutput, calls=%fused_computation.39 | convolution fusion | flops 537395200 | bytes 3145728 | tf_op jit(solution)/shard_map/rmka,rmkb->rmab/dot_general | solution.py:213
  82.1 0.8 fusion.3
  82.9 1.5 %maximum_bitcast_fusion.2 = bf16[2,1,2,512,512]{4,3,2,0,1:T(8,128)(2,1)S(1)} fusion(bf16[1,1,1,2,512,512]{5,4,3,2,1,0:T(8,128)(2,1)S(1)} %get-tuple-element.12, bf16[1,1,1,2,512,512]{5,4,3,2,1,0:T(8,128)(2,1)} %bitcast.22), kind=kLoop, calls=%fused_computation.11 | loop fusion | flops 1048576 | bytes 4194304 | tf_op jit(solution)/shard_map/reshape | solution.py:209
  84.4 1.8 %fusion.2 = bf16[2,1,1,512,512]{4,3,0,2,1:T(8,128)(2,1)S(1)} fusion(bf16[2,1,2,512,512]{4,3,2,0,1:T(8,128)(2,1)S(1)} %maximum_bitcast_fusion.2, bf16[1,1,1,512,512]{4,3,2,1,0:T(8,128)(2,1)S(1)} %copy-done.4, bf16[1,1,1,512,512]{4,3,2,1,0:T(8,128)(2,1)} %bitcast.18), kind=kOutput, calls=%fused_computation.16 | convolution fusion | flops 538443776 | bytes 3145728 | tf_op jit(solution)/shard_map/rmka,rmkb->rmab/dot_general | solution.py:213
  86.2 1.8 %fusion.21 = f32[2,512,512]{2,1,0:T(8,128)S(1)} fusion(bf16[2,1,2,512,512]{4,3,2,0,1:T(8,128)(2,1)S(1)} %maximum_bitcast_fusion.2, bf16[1,1,1,512,512]{4,3,2,1,0:T(8,128)(2,1)S(1)} %copy-done.4, bf16[1,1,1,512,512]{4,3,2,1,0:T(8,128)(2,1)} %bitcast.18), kind=kOutput, calls=%fused_computation.33 | convolution fusion | flops 537395200 | bytes 4194304 | tf_op jit(solution)/shard_map/rmka,rmkb->rmab/dot_general | solution.py:213
  89.0 0.8 fusion.25
  89.7 0.8 fusion.5
  90.5 0.8 fusion.4
  91.9 2.5 %copy.19 = bf16[2,1,4,512,512]{4,3,2,1,0:T(8,128)(2,1)} copy(bf16[2,1,4,512,512]{4,3,0,2,1:T(8,128)(2,1)S(1)} %pad_maximum_fusion) | data formatting | bytes 8388608
  94.4 2.3 %fusion.1 = f32[2,1,512,512]{3,2,1,0:T(8,128)} fusion(f32[1,1,1,512,512]{4,3,1,2,0:T(8,128)S(1)} %get-tuple-element.19, f32[1,1,1,512,512]{4,3,1,2,0:T(8,128)S(1)} %get-tuple-element.18, f32[2,512,512]{2,1,0:T(8,128)S(1)} %fusion.26, f32[2,512,512]{2,1,0:T(8,128)S(1)} %fusion.25, f32[2,512,512]{2,1,0:T(8,128)S(1)} %fusion.22, ...), kind=kOutput, calls=%fused_computation.9 | convolution fusion | flops 539492352 | bytes 11534336 | tf_op jit(solution)/shard_map/rmka,rmkb->rmab/dot_general | solution.py:213
  (31 shorter events, 4.4 us)
Async XLA Ops:
  0.6 7.2 %copy-start.1 = (f32[2,2,512,512]{3,2,1,0:T(8,128)S(1)}, f32[2,2,512,512]{3,2,1,0:T(8,128)}, u32[]{:S(2)}) copy-start(f32[2,2,512,512]{3,2,1,0:T(8,128)} %diag.1) | copy-start | bytes 12582916
  2.5 39.0 %collective-permute-start = (bf16[1,1,512,512]{3,2,1,0:T(8,128)(2,1)S(1)}, bf16[1,1,512,512]{3,2,1,0:T(8,128)(2,1)S(1)}, u32[]{:S(2)}, u32[]{:S(2)}) collective-permute-start(bf16[1,1,512,512]{3,2,1,0:T(8,128)(2,1)S(1)} %get-tuple-element.24), channel_id=1, source_target_pairs={{0,1},{1,2},{2,3},{3,4},{4,5},{5,6},{6,7},{7,0},{8,9},{9,10},{10,1... | collective-permute-start | bytes 1572872 | tf_op jit(solution)/shard_map/ppermute | solution.py:195
  3.0 38.5 %collective-permute-start.1 = (bf16[1,1,512,512]{3,2,1,0:T(8,128)(2,1)S(1)}, bf16[1,1,512,512]{3,2,1,0:T(8,128)(2,1)S(1)}, u32[]{:S(2)}, u32[]{:S(2)}) collective-permute-start(bf16[1,1,512,512]{3,2,1,0:T(8,128)(2,1)S(1)} %get-tuple-element.23), channel_id=1, source_target_pairs={{0,8},{8,16},{16,24},{24,0},{1,9},{9,17},{17,25},{25,1},{2,10},{10... | collective-permute-start | bytes 1572872 | tf_op jit(solution)/shard_map/ppermute | solution.py:195
  5.7 35.7 %copy-start = (bf16[2,2,512,512]{3,2,1,0:T(8,128)(2,1)S(1)}, bf16[2,2,512,512]{3,2,1,0:T(8,128)(2,1)}, u32[]{:S(2)}) copy-start(bf16[2,2,512,512]{3,2,1,0:T(8,128)(2,1)} %up.1) | copy-start | bytes 6291460
  5.7 35.7 %copy-start.2 = (bf16[2,2,512,512]{3,2,1,0:T(8,128)(2,1)S(1)}, bf16[2,2,512,512]{3,2,1,0:T(8,128)(2,1)}, u32[]{:S(2)}) copy-start(bf16[2,2,512,512]{3,2,1,0:T(8,128)(2,1)} %horizontal.1) | copy-start | bytes 6291460
  5.7 52.1 %collective-permute-start.5 = (bf16[2,512,512]{2,1,0:T(8,128)(2,1)S(1)}, bf16[2,512,512]{2,1,0:T(8,128)(2,1)S(1)}, u32[]{:S(2)}, u32[]{:S(2)}) collective-permute-start(bf16[2,512,512]{2,1,0:T(8,128)(2,1)S(1)} %pad_maximum_fusion.2), channel_id=1, source_target_pairs={{0,24},{8,0},{16,8},{24,16},{1,25},{9,1},{17,9},{25,17},{2,26},{10... | collective-permute-start | bytes 3145736 | tf_op jit(solution)/shard_map/ppermute | solution.py:195
  39.4 17.4 %collective-permute-start.3 = (bf16[1,2,10,128,128]{4,3,2,1,0:T(8,128)(2,1)S(1)}, bf16[1,2,10,128,128]{4,3,2,1,0:T(8,128)(2,1)S(1)}, u32[]{:S(2)}, u32[]{:S(2)}) collective-permute-start(bf16[1,2,10,128,128]{4,3,2,1,0:T(8,128)(2,1)S(1)} %slice.81), channel_id=1, source_target_pairs={{0,24},{8,0},{16,8},{24,16},{1,25},{9,1},{17,9},{25,17},{2,26},{10... | collective-permute-start | bytes 1966088 | tf_op jit(solution)/shard_map/ppermute | solution.py:195
  46.3 23.6 %copy-start.3 = (bf16[1,1,1,512,512]{4,3,2,1,0:T(8,128)(2,1)}, bf16[1,1,1,512,512]{4,3,2,1,0:T(8,128)(2,1)S(1)}, u32[]{:S(2)}) copy-start(bf16[1,1,1,512,512]{4,3,2,1,0:T(8,128)(2,1)S(1)} %get-tuple-element.15) | copy-start | bytes 1572868
  46.3 23.6 %collective-permute-start.7 = (bf16[1,1,512,512]{3,2,1,0:T(8,128)(2,1)}, bf16[1,1,512,512]{3,2,1,0:T(8,128)(2,1)}, u32[]{:S(2)}, u32[]{:S(2)}) collective-permute-start(bf16[1,1,512,512]{3,2,1,0:T(8,128)(2,1)} %get-tuple-element.16), channel_id=1, source_target_pairs={{0,7},{1,0},{2,1},{3,2},{4,3},{5,4},{6,5},{7,6},{8,15},{9,8},{10,9... | collective-permute-start | bytes 1572872 | tf_op jit(solution)/shard_map/ppermute | solution.py:195
  48.0 20.0 %collective-permute-start.4 = (bf16[1,1,512,512]{3,2,1,0:T(8,128)(2,1)S(1)}, bf16[1,1,512,512]{3,2,1,0:T(8,128)(2,1)S(1)}, u32[]{:S(2)}, u32[]{:S(2)}) collective-permute-start(bf16[1,1,512,512]{3,2,1,0:T(8,128)(2,1)S(1)} %collective-permute-done.edge_left), channel_id=1, source_target_pairs={{0,24},{8,0},{16,8},{24,16},{1,25},{9,1},{17,9},{25,17},{2,26},{10... | collective-permute-start | bytes 1572872 | tf_op jit(solution)/shard_map/ppermute | solution.py:195
  48.8 34.1 %collective-permute-start.8 = (bf16[1,1,2,512,512]{4,3,2,1,0:T(8,128)(2,1)S(1)}, bf16[1,1,2,512,512]{4,3,2,1,0:T(8,128)(2,1)}, u32[]{:S(2)}, u32[]{:S(2)}) collective-permute-start(bf16[1,1,2,512,512]{4,3,2,1,0:T(8,128)(2,1)S(1)} %get-tuple-element.10), channel_id=1, source_target_pairs={{0,7},{1,0},{2,1},{3,2},{4,3},{5,4},{6,5},{7,6},{8,15},{9,8},{10,9... | collective-permute-start | bytes 3145736 | tf_op jit(solution)/shard_map/ppermute | solution.py:195
  56.8 23.3 %collective-permute-start.2 = (bf16[1,1,512,512]{3,2,1,0:T(8,128)(2,1)}, bf16[1,1,512,512]{3,2,1,0:T(8,128)(2,1)}, u32[]{:S(2)}, u32[]{:S(2)}) collective-permute-start(bf16[1,1,512,512]{3,2,1,0:T(8,128)(2,1)} %get-tuple-element.14), channel_id=1, source_target_pairs={{0,8},{8,16},{16,24},{24,0},{1,9},{9,17},{17,25},{25,1},{2,10},{10... | collective-permute-start | bytes 1572872 | tf_op jit(solution)/shard_map/ppermute | solution.py:195
  57.8 30.2 %collective-permute-start.6 = (bf16[1,1,2,512,512]{4,3,2,1,0:T(8,128)(2,1)S(1)}, bf16[1,1,2,512,512]{4,3,2,1,0:T(8,128)(2,1)S(1)}, u32[]{:S(2)}, u32[]{:S(2)}) collective-permute-start(bf16[1,1,2,512,512]{4,3,2,1,0:T(8,128)(2,1)S(1)} %get-tuple-element.13), channel_id=1, source_target_pairs={{0,1},{1,2},{2,3},{3,4},{4,5},{5,6},{6,7},{7,0},{8,9},{9,10},{10,1... | collective-permute-start | bytes 3145736 | tf_op jit(solution)/shard_map/ppermute | solution.py:195
  69.9 10.2 %copy-start.5 = (bf16[1,1,512,512]{3,2,1,0:T(8,128)(2,1)S(1)}, bf16[1,1,512,512]{3,2,1,0:T(8,128)(2,1)}, u32[]{:S(2)}) copy-start(bf16[1,1,512,512]{3,2,1,0:T(8,128)(2,1)} %get-tuple-element.17) | copy-start | bytes 1572868
  82.9 1.5 %copy-start.4 = (bf16[1,1,1,512,512]{4,3,2,1,0:T(8,128)(2,1)S(1)}, bf16[1,1,1,512,512]{4,3,2,1,0:T(8,128)(2,1)}, u32[]{:S(2)}) copy-start(bf16[1,1,1,512,512]{4,3,2,1,0:T(8,128)(2,1)} %copy-done.3) | copy-start | bytes 1572868
where the time goes:
time: 96.9 us; the launch traced here: 96.7 us
  Pallas kernels  36.9 us (38%)
  waiting for transfers between devices  22.9 us (24%)
  matrix products  13.7 us (14%)
  starting transfers between devices  13.6 us (14%)
  local copies, waits for them, and re-layouts  6.21 us (6%)
  other arithmetic  2.44 us (3%)
    pallas_call x1, Pallas kernels, factored(): pl.pallas_call(factor_kernel, out_shape=(jax.ShapeDtypeStruct(whole, jnp....  31.5 us
    ppermute x9, waiting for transfers between devices, passed_along(): lax.ppermute(value, axis, [(i, (i + by) % size) for i in range(size)])  22.9 us
    dot_general x10, matrix products, gram_term(): jnp.einsum('rmka,rmkb->rmab', former, latter, preferred_element_type=jnp....  13.7 us
    ppermute x9, starting transfers between devices, passed_along(): lax.ppermute(value, axis, [(i, (i + by) % size) for i in range(size)])  13.6 us
    pallas_call x2, Pallas kernels, solved_with(): pl.pallas_call(kernel, out_shape=jax.ShapeDtypeStruct((count, 1, 4, order...  5.42 us
    unnamed x13, local copies, waits for them, and re-layouts  2.51 us
  transfers between devices with their start and end apart: 9, of which 3 were waited for; matrix products, arithmetic and copies ran while one was open for 12% of the time, Pallas kernels for 38%

commit v1 on v0

v1 whole, which is shorter than its diff:
```python
import functools

import jax
import jax.numpy as jnp
from jax import lax
from jax.experimental import pallas as pl
from jax.experimental.pallas import tpu as pltpu
from jax.sharding import PartitionSpec as P

PANEL = 128
STRIP = 16
HALF = 256
MESH = pl.DeviceIdType.MESH
VMEM = pl.BlockSpec(memory_space=pltpu.VMEM)
ANY = pl.BlockSpec(memory_space=pl.ANY)
TN = (((0,), (0,)), ((), ()))


def split(value):
    high = value.astype(jnp.bfloat16)
    low = (value - high.astype(jnp.float32)).astype(jnp.bfloat16)
    return high, low


def product(left, right):
    dot = functools.partial(jnp.dot, preferred_element_type=jnp.float32)
    (lh, ll), (rh, rl) = left, right
    return dot(lh, rh) + (dot(lh, rl) + dot(ll, rh))


def factor_diagonal(work, count):
    lane = lax.broadcasted_iota(jnp.int32, (STRIP, PANEL), 1)
    sub = lax.broadcasted_iota(jnp.int32, (STRIP, PANEL), 0)
    sub_wide = lax.broadcasted_iota(jnp.int32, (STRIP, 2 * PANEL), 0)

    def strip(b, carry):
        start = pl.multiple_of(b * STRIP, STRIP)
        rows = [work[m, pl.ds(start, STRIP), :] for m in range(count)]
        columns = [
            [
                jnp.take_along_axis(rows[m][:, :PANEL], jnp.full_like(lane, start + c), axis=1)
                for c in range(STRIP)
            ]
            for m in range(count)
        ]
        for j in range(STRIP):
            for m in range(count):
                column = columns[m][j]
                pivot = jnp.broadcast_to(column[j : j + 1], column.shape)
                root = lax.rsqrt(pivot)
                square = root * root
                below = jnp.where(sub > j, column, 0.0)
                for c in range(j + 1, STRIP):
                    across = jnp.broadcast_to(columns[m][c][j : j + 1], column.shape)
                    columns[m][c] = columns[m][c] - (below * across) * square
                row = jnp.broadcast_to(rows[m][j : j + 1], rows[m].shape)
                wide_below = jnp.concatenate([below * square] * 2, 1)
                wide_root = jnp.concatenate([root] * 2, 1)
                rows[m] = jnp.where(sub_wide == j, row * wide_root, rows[m] - wide_below * row)
        for m in range(count):
            work[m, pl.ds(start, STRIP), :] = rows[m]
            high = rows[m].astype(jnp.bfloat16).astype(jnp.float32)
            low = rows[m] - high
            after = lane >= start + STRIP
            left_high = jnp.where(after, high[:, :PANEL], 0.0)
            left_low = jnp.where(after, low[:, :PANEL], 0.0)
            left = jnp.concatenate([left_high, left_high, left_low, left_low], 0)
            right = jnp.concatenate([high, low, high, low], 0)
            work[m] = work[m] - lax.dot_general(
                left.T.astype(jnp.bfloat16),
                right.astype(jnp.bfloat16),
                (((1,), (0,)), ((), ())),
                preferred_element_type=jnp.float32,
            )
        return carry

    lax.fori_loop(0, PANEL // STRIP, strip, 0)


def triangle(order):
    return [(p, q) for p in range(order // PANEL) for q in range(p + 1)]


def factor_reds(blocks, factor, inverse, work, packed):
    count, order = blocks.shape[0], blocks.shape[2]
    row = lax.broadcasted_iota(jnp.int32, (PANEL, PANEL), 0)
    col = lax.broadcasted_iota(jnp.int32, (PANEL, PANEL), 1)
    eye = jnp.where(row == col, 1.0, 0.0).astype(jnp.float32)
    inverse[...] = jnp.zeros_like(inverse)
    factor[...] = jnp.zeros_like(factor)
    for start in range(0, order, PANEL):
        stop = start + PANEL
        here = slice(start, stop)
        for m in range(count):
            work[m, :, :PANEL] = blocks[m, here, here]
            work[m, :, PANEL:] = eye
        factor_diagonal(work, count)
        for m in range(count):
            upper = jnp.where(col >= row, work[m, :, :PANEL], 0.0)
            factor[m, here, here] = upper.T
            small = jnp.where(col <= row, work[m, :, PANEL:], 0.0)
            small_parts = split(small)
            if start:
                inverse[m, here, :start] = product(small_parts, split(inverse[m, here, :start]))
            inverse[m, here, here] = small
            if stop < order:
                across = product(small_parts, split(blocks[m, here, stop:]))
                down = across.T
                factor[m, stop:, here] = down
                down_parts = split(down)
                blocks[m, stop:, stop:] -= product(down_parts, split(across))
                inverse[m, stop:, :stop] -= product(down_parts, split(inverse[m, here, :stop]))
    for m in range(count):
        for n, (p, q) in enumerate(triangle(order)):
            tile = inverse[m, p * PANEL : (p + 1) * PANEL, q * PANEL : (q + 1) * PANEL]
            packed[m, n] = tile.astype(jnp.bfloat16)


def solve(packed, coupling, flipped, out):
    order = coupling.shape[0]
    axes = (((1,), (1 if flipped else 0,)), ((), ()))
    n = 0
    for p in range(order // PANEL):
        tiles = [packed[n + q] for q in range(p + 1)]
        n += p + 1
        stop = (p + 1) * PANEL
        left = jnp.concatenate(tiles, 1) if p else tiles[0]
        right = coupling[:, :stop] if flipped else coupling[:stop, :]
        value = lax.dot_general(left, right, axes, preferred_element_type=jnp.float32)
        out[p * PANEL : stop, :] = value.astype(jnp.bfloat16)


def grams(order, terms):
    def body(step, carry):
        rows = pl.ds(pl.multiple_of(step * HALF, HALF), HALF)
        for pairs, emit in terms:
            total = None
            for left, right in pairs:
                value = lax.dot_general(
                    left[:, rows], right[...], TN, preferred_element_type=jnp.float32
                )
                total = value if total is None else total + value
            emit(rows, total)
        return carry

    lax.fori_loop(0, order // HALF, body, 0)


def symmetric_tiles(solved, packed):
    order = solved.shape[0]
    n = 0
    for p in range(order // PANEL):
        stop = (p + 1) * PANEL
        value = lax.dot_general(
            solved[:, p * PANEL : stop],
            solved[:, :stop],
            TN,
            preferred_element_type=jnp.float32,
        )
        for q in range(p + 1):
            packed[n] = value[:, q * PANEL : (q + 1) * PANEL].astype(jnp.bfloat16)
            n += 1


def subtract_symmetric(packed, out):
    for n, (p, q) in enumerate(triangle(out.shape[0])):
        rows = slice(p * PANEL, (p + 1) * PANEL)
        cols = slice(q * PANEL, (q + 1) * PANEL)
        tile = packed[n].astype(jnp.float32)
        out[rows, cols] -= tile
        if p != q:
            out[cols, rows] -= tile.T


def subtract_into(out):
    def emit(rows, total):
        out[rows, :] -= total

    return emit


def negate_into(out):
    def emit(rows, total):
        out[rows, :] = (-total).astype(jnp.bfloat16)

    return emit


def negate_with(extra, out):
    def emit(rows, total):
        out[rows, :] = (-(total + extra[rows, :].astype(jnp.float32))).astype(jnp.bfloat16)

    return emit


def whole_kernel(
    diag, hor, ver,
    factor, schur, links,
    blocks, inverse, work, packed, flat, upright,
    from_up, from_right, inv_up, inv_right, own, own_right, near, near_up,
    give_sym, give_cross, got_left_sym, got_left_cross, got_above,
    local, send, recv,
):
    order = blocks.shape[1]
    r, c = lax.axis_index("row"), lax.axis_index("col")
    rows, cols = lax.axis_size("row"), lax.axis_size("col")
    above, beneath = lax.rem(r + rows - 1, rows), lax.rem(r + 1, rows)
    left, right = lax.rem(c + cols - 1, cols), lax.rem(c + 1, cols)
    loads = [
        pltpu.make_async_copy(diag.at[0, 0], blocks.at[0], local.at[0]),
        pltpu.make_async_copy(diag.at[1, 1], blocks.at[1], local.at[1]),
        pltpu.make_async_copy(diag.at[0, 1], schur.at[0], local.at[2]),
        pltpu.make_async_copy(diag.at[1, 0], schur.at[1], local.at[3]),
        pltpu.make_async_copy(hor, flat, local.at[4]),
        pltpu.make_async_copy(ver, upright, local.at[5]),
    ]
    barrier = pltpu.get_barrier_semaphore()
    peers = [(above, c), (beneath, c), (r, left), (r, right), (above, right), (beneath, left)]
    for peer in peers:
        pl.semaphore_signal(barrier, inc=1, device_id=peer, device_id_type=MESH)
    for load in loads:
        load.start()
    pl.semaphore_wait(barrier, len(peers))

    def remote(src, dst, k, peer):
        copy = pltpu.make_async_remote_copy(
            src_ref=src, dst_ref=dst, send_sem=send.at[k], recv_sem=recv.at[k],
            device_id=peer, device_id_type=MESH,
        )
        copy.start()
        return copy

    sent = [
        remote(ver.at[0, 0], from_up.at[0], 0, (above, c)),
        remote(hor.at[0, 0], from_up.at[1], 1, (above, c)),
        remote(hor.at[0, 1], from_up.at[2], 2, (above, right)),
        remote(ver.at[0, 0], from_right.at[0], 3, (r, left)),
        remote(hor.at[0, 0], from_right.at[1], 4, (r, left)),
    ]
    loads[0].wait()
    loads[1].wait()
    factor_reds(blocks, factor, inverse, work, packed)
    for load in loads[2:]:
        load.wait()
    U, L, D, R = (slice(k * order, (k + 1) * order) for k in range(4))
    for at, coupling, flipped in (
        (D, upright.at[1, 1], False),
        (R, flat.at[1, 1], False),
    ):
        solve(packed.at[1], coupling, flipped, own.at[:, at])
    sent.append(remote(packed.at[0], inv_up, 5, (above, c)))
    sent.append(remote(packed.at[0], inv_right, 6, (r, left)))
    symmetric_tiles(own.at[:, D], give_sym.at[0])
    symmetric_tiles(own.at[:, R], give_sym.at[1])

    def give(rows, total):
        give_cross[rows, :] = total.astype(jnp.bfloat16)

    grams(order, [([(own.at[:, R], own.at[:, D])], give)])
    solve(packed.at[1], upright.at[0, 1], True, own.at[:, U])
    sent.append(remote(give_sym.at[0], got_above, 7, (beneath, c)))
    sent.append(remote(give_sym.at[1], got_left_sym, 8, (r, right)))
    sent.append(remote(give_cross, got_left_cross, 9, (r, right)))
    solve(packed.at[1], flat.at[1, 0], True, own.at[:, L])
    first, second = slice(0, order), slice(order, 2 * order)
    solve(packed.at[0], upright.at[0, 0], False, own_right.at[:, first])
    solve(packed.at[0], flat.at[0, 0], False, own_right.at[:, second])
    down, across = own_right.at[:, first], own_right.at[:, second]
    up_, left_, down_, right_ = (own.at[:, at] for at in (U, L, D, R))
    grams(
        order,
        [
            ([(across, across), (up_, up_)], subtract_into(schur.at[0])),
            ([(up_, down_)], negate_into(links.at[0, 1])),
            ([(across, down), (up_, left_)], negate_into(links.at[0, 3])),
            ([(down, down), (left_, left_)], subtract_into(schur.at[1])),
            ([(left_, right_)], negate_into(links.at[1, 0])),
        ],
    )
    sent[3].wait_recv()
    sent[4].wait_recv()
    sent[6].wait_recv()
    near_left, near_down, near_right = (near.at[:, k * order : (k + 1) * order] for k in range(3))
    solve(inv_right, flat.at[0, 1], True, near_left)
    solve(inv_right, from_right.at[0], False, near_down)
    solve(inv_right, from_right.at[1], False, near_right)
    grams(
        order,
        [
            ([(near_left, near_left)], subtract_into(schur.at[0])),
            ([(near_left, near_right)], negate_into(links.at[0, 0])),
            ([(up_, right_), (near_left, near_down)], negate_into(links.at[0, 2])),
        ],
    )
    sent[8].wait_recv()
    subtract_symmetric(got_left_sym, schur.at[1])
    sent[9].wait_recv()
    sent[0].wait_recv()
    sent[1].wait_recv()
    sent[2].wait_recv()
    sent[5].wait_recv()
    below_up, below_left, below_down, below_right = (near_up.at[:, at] for at in (U, L, D, R))
    solve(inv_up, upright.at[1, 0], True, below_up)
    solve(inv_up, from_up.at[2], True, below_left)
    solve(inv_up, from_up.at[0], False, below_down)
    solve(inv_up, from_up.at[1], False, below_right)
    grams(
        order,
        [
            ([(below_up, below_up)], subtract_into(schur.at[1])),
            ([(below_up, below_down)], negate_into(links.at[1, 1])),
            ([(left_, down_), (below_up, below_right)], negate_into(links.at[1, 2])),
            ([(below_up, below_left)], negate_with(got_left_cross, links.at[1, 3])),
        ],
    )
    sent[7].wait_recv()
    subtract_symmetric(got_above, schur.at[0])
    for copy in sent:
        copy.wait_send()


def on_device(diag_blocks, horizontal, vertical):
    order = diag_blocks.shape[-1]
    assert diag_blocks.shape[:2] == (2, 2)
    tiles = len(triangle(order))
    square = (order, order)
    bf16, f32 = jnp.bfloat16, jnp.float32
    packed = (tiles, PANEL, PANEL)
    factor, schur, links = pl.pallas_call(
        whole_kernel,
        out_shape=(
            jax.ShapeDtypeStruct((2,) + square, f32),
            jax.ShapeDtypeStruct((2,) + square, f32),
            jax.ShapeDtypeStruct((2, 4) + square, bf16),
        ),
        in_specs=[ANY] * 3,
        out_specs=(VMEM, VMEM, VMEM),
        scratch_shapes=[
            pltpu.VMEM((2,) + square, f32),
            pltpu.VMEM((2,) + square, f32),
            pltpu.VMEM((2, PANEL, 2 * PANEL), f32),
            pltpu.VMEM((2,) + packed, bf16),
            pltpu.VMEM((2, 2) + square, bf16),
            pltpu.VMEM((2, 2) + square, bf16),
            pltpu.VMEM((3,) + square, bf16),
            pltpu.VMEM((2,) + square, bf16),
            pltpu.VMEM(packed, bf16),
            pltpu.VMEM(packed, bf16),
            pltpu.VMEM((order, 4 * order), bf16),
            pltpu.VMEM((order, 2 * order), bf16),
            pltpu.VMEM((order, 3 * order), bf16),
            pltpu.VMEM((order, 4 * order), bf16),
            pltpu.VMEM((2,) + packed, bf16),
            pltpu.VMEM(square, bf16),
            pltpu.VMEM(packed, bf16),
            pltpu.VMEM(square, bf16),
            pltpu.VMEM(packed, bf16),
            pltpu.SemaphoreType.DMA((6,)),
            pltpu.SemaphoreType.DMA((10,)),
            pltpu.SemaphoreType.DMA((10,)),
        ],
        compiler_params=pltpu.CompilerParams(
            collective_id=0, has_side_effects=True, vmem_limit_bytes=44 * 2**20
        ),
        cost_estimate=pl.CostEstimate(
            flops=20_000_000_000, bytes_accessed=8 * diag_blocks.size, transcendentals=0
        ),
    )(diag_blocks, horizontal, vertical)
    return (factor[:, None], schur[:, None], links[:, None])


def solution(mesh):
    in_specs = (
        P("row", "col", None, None),
        P("row", "col", None, None),
        P("row", "col", None, None),
    )
    out_specs = (
        P("row", "col", None, None),
        P("row", "col", None, None),
        P("row", "col", None, None, None),
    )
    return jax.shard_map(
        on_device, mesh=mesh, in_specs=in_specs, out_specs=out_specs, check_vma=False
    )
```

time: 96.9 us -> 68 us (0.70)
  waiting for transfers between devices: 22.9 us -> 0 us
  Pallas kernels: 36.9 us -> 57.6 us
  matrix products: 13.7 us -> 0 us
  starting transfers between devices: 13.6 us -> 0 us
  local copies, waits for them, and re-layouts: 6.21 us -> 9.45 us
  other arithmetic: 2.44 us -> 0 us
    ppermute x9 -> x0, waiting for transfers between devices: 22.9 us -> none  [passed_along(): lax.ppermute(value, axis, [(i, (i + by) % size) for i in range(size)])]
    pallas_call x3 -> x1, Pallas kernels: 36.9 us -> 57.6 us  [on_device(): pl.pallas_call(whole_kernel, out_shape=(jax.ShapeDtypeStruct((2,) + squar...]
    dot_general x10 -> x0, matrix products: 13.7 us -> none  [gram_term(): jnp.einsum('rmka,rmkb->rmab', former, latter, preferred_element_type=jnp....]
    ppermute x9 -> x0, starting transfers between devices: 13.6 us -> none  [passed_along(): lax.ppermute(value, axis, [(i, (i + by) % size) for i in range(size)])]
    unnamed x13 -> x9, local copies, waits for them, and re-layouts: 2.51 us -> 9.45 us
    another operation x2 -> x0, local copies, waits for them, and re-layouts: 1.98 us -> none  [the longest x1 1.81 us: on_device(): jnp.stack([horizontal[0, 0], vertical[0, 0]])]
    reshape x2 -> x0, other arithmetic: 1.67 us -> none  [combine_rows(): return joined.reshape((2 * even_rows.shape[0],) + even_rows.shape[1:])]
    squeeze x1 -> x0, local copies, waits for them, and re-layouts: 1.18 us -> none  [on_device(): got_above = passed_along(solved[-1:, :, 3], 'row', 1)]
  transfers between devices with their start and end apart: 9 -> 0, of which waited for: 3 -> 0; matrix products, arithmetic and copies ran while one was open for 12% -> 0% of each run, Pallas kernels for 38% -> 0%
where the time goes in v1:
time: 68 us; the launch traced here: 67.7 us
  Pallas kernels  57.6 us (85%)
  local copies, waits for them, and re-layouts  9.45 us (14%)
    pallas_call x1, Pallas kernels, on_device(): pl.pallas_call(whole_kernel, out_shape=(jax.ShapeDtypeStruct((2,) + squar...  57.6 us
    unnamed x9, local copies, waits for them, and re-layouts  9.45 us

profile of v1, /device:TPU:0, one launch (start us, length us, event | category | flops | bytes accessed | tf_op | source)
XLA Modules:
  0.0 67.7 jit_solution(4454876346291164721)
XLA Ops:
  0.6 0.0 copy-start
  0.6 1.6 %copy-done = bf16[2,2,512,512]{3,2,1,0:T(8,128)(2,1)S(1)} copy-done((bf16[2,2,512,512]{3,2,1,0:T(8,128)(2,1)S(1)}, bf16[2,2,512,512]{3,2,1,0:T(8,128)(2,1)}, u32[]{:S(2)}) %copy-start) | copy-done | bytes 2097176
  2.2 0.0 copy-start.1
  2.2 1.6 %copy-done.1 = bf16[2,2,512,512]{3,2,1,0:T(8,128)(2,1)S(1)} copy-done((bf16[2,2,512,512]{3,2,1,0:T(8,128)(2,1)S(1)}, bf16[2,2,512,512]{3,2,1,0:T(8,128)(2,1)}, u32[]{:S(2)}) %copy-start.1) | copy-done | bytes 2097176
  3.8 57.6 %shard_map.58 = (f32[2,512,512]{2,1,0:T(8,128)S(1)}, f32[2,512,512]{2,1,0:T(8,128)S(1)}, bf16[2,4,512,512]{3,2,1,0:T(8,128)(2,1)}) custom-call(f32[2,2,512,512]{3,2,1,0:T(8,128)} %diag.1, bf16[2,2,512,512]{3,2,1,0:T(8,128)(2,1)S(1)} %copy-done, bf16[2,2,512,512]{3,2,1,0:T(8,128)(2,1)S(1)} %copy-done.1), custom_call_target="tpu_custom_call" | custom-call | flops 20000000000 | bytes 8388608 | tf_op jit(solution)/shard_map/pallas_call | solution.py:329
  61.5 1.3 %copy.12 = f32[2,1,512,512]{3,2,1,0:T(8,128)} copy(f32[2,1,512,512]{3,2,1,0:T(8,128)S(1)} %bitcast.10) | data formatting | bytes 4194304
  62.8 0.0 copy-start.2
  62.8 1.3 %copy.13 = f32[2,1,512,512]{3,2,1,0:T(8,128)} copy(f32[2,1,512,512]{3,2,1,0:T(8,128)S(1)} %bitcast.9) | data formatting | bytes 4194304
  64.1 1.6 %copy-done.2 = bf16[2,4,512,512]{3,2,1,0:T(8,128)(2,1)S(1)} copy-done((bf16[2,4,512,512]{3,2,1,0:T(8,128)(2,1)S(1)}, bf16[2,4,512,512]{3,2,1,0:T(8,128)(2,1)}, u32[]{:S(2)}) %copy-start.2) | copy-done | bytes 4194328
  65.7 2.0 %copy.14 = bf16[2,1,4,512,512]{4,3,2,1,0:T(8,128)(2,1)} copy(bf16[2,1,4,512,512]{4,3,2,1,0:T(8,128)(2,1)S(1)} %bitcast.11) | data formatting | bytes 8388608
Async XLA Ops:
  0.6 1.6 %copy-start = (bf16[2,2,512,512]{3,2,1,0:T(8,128)(2,1)S(1)}, bf16[2,2,512,512]{3,2,1,0:T(8,128)(2,1)}, u32[]{:S(2)}) copy-start(bf16[2,2,512,512]{3,2,1,0:T(8,128)(2,1)} %hor.1) | copy-start | bytes 6291460
  2.2 1.6 %copy-start.1 = (bf16[2,2,512,512]{3,2,1,0:T(8,128)(2,1)S(1)}, bf16[2,2,512,512]{3,2,1,0:T(8,128)(2,1)}, u32[]{:S(2)}) copy-start(bf16[2,2,512,512]{3,2,1,0:T(8,128)(2,1)} %ver.1) | copy-start | bytes 6291460
  62.8 2.9 %copy-start.2 = (bf16[2,4,512,512]{3,2,1,0:T(8,128)(2,1)S(1)}, bf16[2,4,512,512]{3,2,1,0:T(8,128)(2,1)}, u32[]{:S(2)}) copy-start(bf16[2,4,512,512]{3,2,1,0:T(8,128)(2,1)} %get-tuple-element.8) | copy-start | bytes 12582916

commit v2 on v1

--- a/solution.py
+++ b/solution.py
@@ -10,9 +10,10 @@
 PANEL = 128
 STRIP = 16
 HALF = 256
+ROW_TILE = 16
 MESH = pl.DeviceIdType.MESH
 VMEM = pl.BlockSpec(memory_space=pltpu.VMEM)
-ANY = pl.BlockSpec(memory_space=pl.ANY)
+HBM = pl.BlockSpec(memory_space=pltpu.HBM)
 TN = (((0,), (0,)), ((), ()))
 
 
@@ -113,21 +114,91 @@
     for m in range(count):
         for n, (p, q) in enumerate(triangle(order)):
             tile = inverse[m, p * PANEL : (p + 1) * PANEL, q * PANEL : (q + 1) * PANEL]
-            packed[m, n] = tile.astype(jnp.bfloat16)
-
-
-def solve(packed, coupling, flipped, out):
-    order = coupling.shape[0]
+            packed[m, 0, n], packed[m, 1, n] = split(tile)
+
+
+def triangle_index(p, q):
+    return p * (p + 1) // 2 + q
+
+
+def off_diagonal(order):
+    return [(p, q) for p, q in triangle(order) if p != q]
+
+
+def grid_of_panel():
+    row = lax.broadcasted_iota(jnp.int32, (PANEL, PANEL), 0)
+    col = lax.broadcasted_iota(jnp.int32, (PANEL, PANEL), 1)
+    return row, col
+
+
+def compact_rows(order):
+    panels = order // PANEL
+    return (len(off_diagonal(order)) + panels // 2) * PANEL + ROW_TILE
+
+
+def tile_rows(n):
+    return slice(n * PANEL, (n + 1) * PANEL)
+
+
+def compact(tile_of, order, out, flip):
+    row, col = grid_of_panel()
+    pairs = off_diagonal(order)
+    for n, (p, q) in enumerate(pairs):
+        out[tile_rows(n), :] = tile_of(p, q).astype(jnp.bfloat16)
+    lines = []
+    for k in range(0, order // PANEL, 2):
+        first, second = tile_of(k, k), tile_of(k + 1, k + 1)
+        other = second.T if flip else second
+        joined = jnp.where(row >= col, first, other)
+        out[tile_rows(len(pairs) + k // 2), :] = joined.astype(jnp.bfloat16)
+        lines.append(jnp.sum(jnp.where(row == col, second, 0.0), axis=0, keepdims=True))
+    lines.append(jnp.zeros((ROW_TILE - len(lines), PANEL), jnp.float32))
+    base = compact_rows(order) - ROW_TILE
+    out[base:, :] = jnp.concatenate(lines, 0).astype(jnp.bfloat16)
+
+
+def spread_diagonal(packed, order, symmetric):
+    row, col = grid_of_panel()
+    skip = len(off_diagonal(order))
+    base = compact_rows(order) - ROW_TILE
+    lines = packed[base:, :].astype(jnp.float32)
+    tiles = []
+    for k in range(order // PANEL // 2):
+        joined = packed[tile_rows(skip + k), :].astype(jnp.float32)
+        turned = joined.T
+        line = jnp.broadcast_to(lines[k : k + 1, :], joined.shape)
+        tiles.append(jnp.where(row >= col, joined, turned if symmetric else 0.0))
+        upper = joined if symmetric else 0.0
+        tiles.append(jnp.where(row == col, line, jnp.where(col < row, turned, upper)))
+    return tiles
+
+
+def solve(parts, coupling, flipped, out, columns=None):
+    order = out.shape[0]
     axes = (((1,), (1 if flipped else 0,)), ((), ()))
-    n = 0
     for p in range(order // PANEL):
-        tiles = [packed[n + q] for q in range(p + 1)]
-        n += p + 1
         stop = (p + 1) * PANEL
-        left = jnp.concatenate(tiles, 1) if p else tiles[0]
         right = coupling[:, :stop] if flipped else coupling[:stop, :]
-        value = lax.dot_general(left, right, axes, preferred_element_type=jnp.float32)
+        value = None
+        for tile_of in parts:
+            tiles = [tile_of(p, q) for q in range(p + 1)]
+            left = jnp.concatenate(tiles, 1) if p else tiles[0]
+            term = lax.dot_general(left, right, axes, preferred_element_type=jnp.float32)
+            value = term if value is None else value + term
         out[p * PANEL : stop, :] = value.astype(jnp.bfloat16)
+
+
+def own_parts(packed, m):
+    return [
+        lambda p, q, part=part: packed[m, part, triangle_index(p, q)] for part in range(2)
+    ]
+
+
+def far_parts(packed, diagonal, order):
+    for k, tile in enumerate(spread_diagonal(packed, order, False)):
+        diagonal[k] = tile.astype(jnp.bfloat16)
+    place = {pair: n for n, pair in enumerate(off_diagonal(order))}
+    return [lambda p, q: diagonal[p] if p == q else packed[tile_rows(place[p, q]), :]]
 
 
 def grams(order, terms):
@@ -146,30 +217,28 @@
     lax.fori_loop(0, order // HALF, body, 0)
 
 
-def symmetric_tiles(solved, packed):
+def compact_gram(solved, out):
     order = solved.shape[0]
-    n = 0
-    for p in range(order // PANEL):
-        stop = (p + 1) * PANEL
-        value = lax.dot_general(
-            solved[:, p * PANEL : stop],
-            solved[:, :stop],
+    strips = [
+        lax.dot_general(
+            solved[:, tile_rows(p)],
+            solved[:, : (p + 1) * PANEL],
             TN,
             preferred_element_type=jnp.float32,
         )
-        for q in range(p + 1):
-            packed[n] = value[:, q * PANEL : (q + 1) * PANEL].astype(jnp.bfloat16)
-            n += 1
-
-
-def subtract_symmetric(packed, out):
-    for n, (p, q) in enumerate(triangle(out.shape[0])):
-        rows = slice(p * PANEL, (p + 1) * PANEL)
-        cols = slice(q * PANEL, (q + 1) * PANEL)
-        tile = packed[n].astype(jnp.float32)
-        out[rows, cols] -= tile
-        if p != q:
-            out[cols, rows] -= tile.T
+        for p in range(order // PANEL)
+    ]
+    compact(lambda p, q: strips[p][:, tile_rows(q)], order, out, False)
+
+
+def subtract_compact(packed, out):
+    order = out.shape[0]
+    for n, (p, q) in enumerate(off_diagonal(order)):
+        tile = packed[tile_rows(n), :].astype(jnp.float32)
+        out[tile_rows(p), tile_rows(q)] -= tile
+        out[tile_rows(q), tile_rows(p)] -= tile.T
+    for k, tile in enumerate(spread_diagonal(packed, order, True)):
+        out[tile_rows(k), tile_rows(k)] -= tile
 
 
 def subtract_into(out):
@@ -197,11 +266,13 @@
     diag, hor, ver,
     factor, schur, links,
     blocks, inverse, work, packed, flat, upright,
-    from_up, from_right, inv_up, inv_right, own, own_right, near, near_up,
-    give_sym, give_cross, got_left_sym, got_left_cross, got_above,
+    from_up, from_right, mine, inv_up, inv_right, diag_up, diag_right,
+    own, own_right, near, near_up,
+    give_down, give_sym, give_cross, got_sym, got_cross, got_above,
     local, send, recv,
 ):
     order = blocks.shape[1]
+    half = order // 2
     r, c = lax.axis_index("row"), lax.axis_index("col")
     rows, cols = lax.axis_size("row"), lax.axis_size("col")
     above, beneath = lax.rem(r + rows - 1, rows), lax.rem(r + 1, rows)
@@ -230,43 +301,43 @@
         copy.start()
         return copy
 
-    sent = [
-        remote(ver.at[0, 0], from_up.at[0], 0, (above, c)),
-        remote(hor.at[0, 0], from_up.at[1], 1, (above, c)),
-        remote(hor.at[0, 1], from_up.at[2], 2, (above, right)),
-        remote(ver.at[0, 0], from_right.at[0], 3, (r, left)),
-        remote(hor.at[0, 0], from_right.at[1], 4, (r, left)),
-    ]
+    down_up = remote(ver.at[0, 0], from_up.at[0], 0, (above, c))
+    right_up = remote(hor.at[0, 0], from_up.at[1], 1, (above, c))
+    left_up = [remote(hor.at[0, 1, :half], from_up.at[2, :half], 2, (above, right))]
+    down_right = remote(ver.at[0, 0], from_right.at[0], 3, (r, left))
+    right_right = remote(hor.at[0, 0], from_right.at[1], 4, (r, left))
     loads[0].wait()
     loads[1].wait()
     factor_reds(blocks, factor, inverse, work, packed)
     for load in loads[2:]:
         load.wait()
+    compact(
+        lambda p, q: inverse[0, tile_rows(p), tile_rows(q)], order, mine, True
+    )
     U, L, D, R = (slice(k * order, (k + 1) * order) for k in range(4))
-    for at, coupling, flipped in (
-        (D, upright.at[1, 1], False),
-        (R, flat.at[1, 1], False),
-    ):
-        solve(packed.at[1], coupling, flipped, own.at[:, at])
-    sent.append(remote(packed.at[0], inv_up, 5, (above, c)))
-    sent.append(remote(packed.at[0], inv_right, 6, (r, left)))
-    symmetric_tiles(own.at[:, D], give_sym.at[0])
-    symmetric_tiles(own.at[:, R], give_sym.at[1])
+    up_, left_, down_, right_ = (own.at[:, at] for at in (U, L, D, R))
+    one = own_parts(packed, 1)
+    solve(one, upright.at[1, 1], False, down_)
+    inverse_up = remote(mine, inv_up, 5, (above, c))
+    inverse_right = remote(mine, inv_right, 6, (r, left))
+    left_up.append(remote(hor.at[0, 1, half:], from_up.at[2, half:], 10, (above, right)))
+    compact_gram(down_, give_down)
+    solve(one, flat.at[1, 1], False, right_)
+    sent_down = remote(give_down, got_above, 7, (beneath, c))
+    compact_gram(right_, give_sym)
 
     def give(rows, total):
         give_cross[rows, :] = total.astype(jnp.bfloat16)
 
-    grams(order, [([(own.at[:, R], own.at[:, D])], give)])
-    solve(packed.at[1], upright.at[0, 1], True, own.at[:, U])
-    sent.append(remote(give_sym.at[0], got_above, 7, (beneath, c)))
-    sent.append(remote(give_sym.at[1], got_left_sym, 8, (r, right)))
-    sent.append(remote(give_cross, got_left_cross, 9, (r, right)))
-    solve(packed.at[1], flat.at[1, 0], True, own.at[:, L])
-    first, second = slice(0, order), slice(order, 2 * order)
-    solve(packed.at[0], upright.at[0, 0], False, own_right.at[:, first])
-    solve(packed.at[0], flat.at[0, 0], False, own_right.at[:, second])
-    down, across = own_right.at[:, first], own_right.at[:, second]
-    up_, left_, down_, right_ = (own.at[:, at] for at in (U, L, D, R))
+    grams(order, [([(right_, down_)], give)])
+    solve(one, upright.at[0, 1], True, up_)
+    sent_sym = remote(give_sym, got_sym, 8, (r, right))
+    sent_cross = remote(give_cross, got_cross, 9, (r, right))
+    solve(one, flat.at[1, 0], True, left_)
+    zero = own_parts(packed, 0)
+    down, across = own_right.at[:, :order], own_right.at[:, order:]
+    solve(zero, upright.at[0, 0], False, down)
+    solve(zero, flat.at[0, 0], False, across)
     grams(
         order,
         [
@@ -277,13 +348,14 @@
             ([(left_, right_)], negate_into(links.at[1, 0])),
         ],
     )
-    sent[3].wait_recv()
-    sent[4].wait_recv()
-    sent[6].wait_recv()
+    down_right.wait_recv()
+    right_right.wait_recv()
+    inverse_right.wait_recv()
     near_left, near_down, near_right = (near.at[:, k * order : (k + 1) * order] for k in range(3))
-    solve(inv_right, flat.at[0, 1], True, near_left)
-    solve(inv_right, from_right.at[0], False, near_down)
-    solve(inv_right, from_right.at[1], False, near_right)
+    far = far_parts(inv_right, diag_right, order)
+    solve(far, flat.at[0, 1], True, near_left)
+    solve(far, from_right.at[0], False, near_down)
+    solve(far, from_right.at[1], False, near_right)
     grams(
         order,
         [
@@ -292,31 +364,67 @@
             ([(up_, right_), (near_left, near_down)], negate_into(links.at[0, 2])),
         ],
     )
-    sent[8].wait_recv()
-    subtract_symmetric(got_left_sym, schur.at[1])
-    sent[9].wait_recv()
-    sent[0].wait_recv()
-    sent[1].wait_recv()
-    sent[2].wait_recv()
-    sent[5].wait_recv()
+    down_up.wait_recv()
+    right_up.wait_recv()
+    inverse_up.wait_recv()
     below_up, below_left, below_down, below_right = (near_up.at[:, at] for at in (U, L, D, R))
-    solve(inv_up, upright.at[1, 0], True, below_up)
-    solve(inv_up, from_up.at[2], True, below_left)
-    solve(inv_up, from_up.at[0], False, below_down)
-    solve(inv_up, from_up.at[1], False, below_right)
+    far = far_parts(inv_up, diag_up, order)
+    solve(far, upright.at[1, 0], True, below_up)
+    solve(far, from_up.at[0], False, below_down)
+    solve(far, from_up.at[1], False, below_right)
     grams(
         order,
         [
             ([(below_up, below_up)], subtract_into(schur.at[1])),
             ([(below_up, below_down)], negate_into(links.at[1, 1])),
             ([(left_, down_), (below_up, below_right)], negate_into(links.at[1, 2])),
-            ([(below_up, below_left)], negate_with(got_left_cross, links.at[1, 3])),
         ],
     )
-    sent[7].wait_recv()
-    subtract_symmetric(got_above, schur.at[0])
-    for copy in sent:
+    sent_sym.wait_recv()
+    subtract_compact(got_sym, schur.at[1])
+    sent_cross.wait_recv()
+    for k in range(2):
+        part = slice(k * half, (k + 1) * half)
+        left_up[k].wait_recv()
+        solve(far, from_up.at[2, part], True, below_left.at[:, part])
+        grams(
+            order,
+            [
+                (
+                    [(below_up, below_left.at[:, part])],
+                    negate_with(got_cross.at[:, part], links.at[1, 3, :, part]),
+                )
+            ],
+        )
+    sent_down.wait_recv()
+    subtract_compact(got_above, schur.at[0])
+    for copy in (
+        down_up, right_up, *left_up, down_right, right_right,
+        inverse_up, inverse_right, sent_down, sent_sym, sent_cross,
+    ):
         copy.wait_send()
+
+
+def output_kernel(*refs):
+    count = (len(refs) - 1) // 2
+    copies = [
+        pltpu.make_async_copy(refs[k], refs[count + k], refs[-1].at[k]) for k in range(count)
+    ]
+    for copy in copies:
+        copy.start()
+    for copy in copies:
+        copy.wait()
+
+
+def put_out(*arrays):
+    return pl.pallas_call(
+        output_kernel,
+        out_shape=tuple(jax.ShapeDtypeStruct(a.shape, a.dtype) for a in arrays),
+        in_specs=[VMEM] * len(arrays),
+        out_specs=(HBM,) * len(arrays),
+        scratch_shapes=[pltpu.SemaphoreType.DMA((len(arrays),))],
+        compiler_params=pltpu.CompilerParams(vmem_limit_bytes=16 * 2**20),
+    )(*arrays)
 
 
 def on_device(diag_blocks, horizontal, vertical):
@@ -325,47 +433,53 @@
     tiles = len(triangle(order))
     square = (order, order)
     bf16, f32 = jnp.bfloat16, jnp.float32
-    packed = (tiles, PANEL, PANEL)
-    factor, schur, links = pl.pallas_call(
+    dense = (compact_rows(order), PANEL)
+    diagonal = (order // PANEL, PANEL, PANEL)
+    outs = pl.pallas_call(
         whole_kernel,
         out_shape=(
             jax.ShapeDtypeStruct((2,) + square, f32),
             jax.ShapeDtypeStruct((2,) + square, f32),
             jax.ShapeDtypeStruct((2, 4) + square, bf16),
         ),
-        in_specs=[ANY] * 3,
+        in_specs=[HBM] * 3,
         out_specs=(VMEM, VMEM, VMEM),
         scratch_shapes=[
             pltpu.VMEM((2,) + square, f32),
             pltpu.VMEM((2,) + square, f32),
             pltpu.VMEM((2, PANEL, 2 * PANEL), f32),
-            pltpu.VMEM((2,) + packed, bf16),
+            pltpu.VMEM((2, 2, tiles, PANEL, PANEL), bf16),
             pltpu.VMEM((2, 2) + square, bf16),
             pltpu.VMEM((2, 2) + square, bf16),
             pltpu.VMEM((3,) + square, bf16),
             pltpu.VMEM((2,) + square, bf16),
-            pltpu.VMEM(packed, bf16),
-            pltpu.VMEM(packed, bf16),
+            pltpu.VMEM(dense, bf16),
+            pltpu.VMEM(dense, bf16),
+            pltpu.VMEM(dense, bf16),
+            pltpu.VMEM(diagonal, bf16),
+            pltpu.VMEM(diagonal, bf16),
             pltpu.VMEM((order, 4 * order), bf16),
             pltpu.VMEM((order, 2 * order), bf16),
             pltpu.VMEM((order, 3 * order), bf16),
             pltpu.VMEM((order, 4 * order), bf16),
-            pltpu.VMEM((2,) + packed, bf16),
+            pltpu.VMEM(dense, bf16),
+            pltpu.VMEM(dense, bf16),
             pltpu.VMEM(square, bf16),
-            pltpu.VMEM(packed, bf16),
+            pltpu.VMEM(dense, bf16),
             pltpu.VMEM(square, bf16),
-            pltpu.VMEM(packed, bf16),
+            pltpu.VMEM(dense, bf16),
             pltpu.SemaphoreType.DMA((6,)),
-            pltpu.SemaphoreType.DMA((10,)),
-            pltpu.SemaphoreType.DMA((10,)),
+            pltpu.SemaphoreType.DMA((11,)),
+            pltpu.SemaphoreType.DMA((11,)),
         ],
         compiler_params=pltpu.CompilerParams(
-            collective_id=0, has_side_effects=True, vmem_limit_bytes=44 * 2**20
+            collective_id=0, has_side_effects=True, vmem_limit_bytes=42 * 2**20
         ),
         cost_estimate=pl.CostEstimate(
             flops=20_000_000_000, bytes_accessed=8 * diag_blocks.size, transcendentals=0
         ),
-    )(diag_blocks, horizontal, vertical)
+    )(*(pltpu.with_memory_space_constraint(a, pltpu.HBM) for a in (diag_blocks, horizontal, vertical)))
+    factor, schur, links = put_out(*outs)
     return (factor[:, None], schur[:, None], links[:, None])
 
 

time: 68 us -> 57.5 us (0.85)
  local copies, waits for them, and re-layouts: 9.45 us -> 0 us
  Pallas kernels: 57.6 us -> 56.7 us
    unnamed x9 -> x0, local copies, waits for them, and re-layouts: 9.45 us -> none
    pallas_call x1, Pallas kernels: 57.6 us -> 53.3 us  [on_device(): pl.pallas_call(whole_kernel, out_shape=(jax.ShapeDtypeStruct((2,) + squar...]
    pallas_call x0 -> x1, Pallas kernels: none -> 3.42 us  [put_out(): pl.pallas_call(output_kernel, out_shape=tuple((jax.ShapeDtypeStruct(a.sha...]
where the time goes in v2:
time: 57.5 us; the launch traced here: 57.4 us
  Pallas kernels  56.7 us (99%)
  between operations  0.64 us (1%)
    pallas_call x1, Pallas kernels, on_device(): pl.pallas_call(whole_kernel, out_shape=(jax.ShapeDtypeStruct((2,) + squar...  53.3 us
    pallas_call x1, Pallas kernels, put_out(): pl.pallas_call(output_kernel, out_shape=tuple((jax.ShapeDtypeStruct(a.sha...  3.42 us

profile of v2, /device:TPU:0, one launch (start us, length us, event | category | flops | bytes accessed | tf_op | source)
XLA Modules:
  0.0 57.4 jit_solution(11700871216700057451)
XLA Ops:
  0.6 53.3 %shard_map.58 = (f32[2,512,512]{2,1,0:T(8,128)S(1)}, f32[2,512,512]{2,1,0:T(8,128)S(1)}, bf16[2,4,512,512]{3,2,1,0:T(8,128)(2,1)S(1)}) custom-call(f32[2,2,512,512]{3,2,1,0:T(8,128)} %diag.1, bf16[2,2,512,512]{3,2,1,0:T(8,128)(2,1)} %hor.1, bf16[2,2,512,512]{3,2,1,0:T(8,128)(2,1)} %ver.1), custom_call_target="tpu_custom_call" | custom-call | flops 20000000000 | bytes 8388608 | tf_op jit(solution)/shard_map/pallas_call | solution.py:438
  53.9 3.4 %shard_map.59 = (f32[2,512,512]{2,1,0:T(8,128)}, f32[2,512,512]{2,1,0:T(8,128)}, bf16[2,4,512,512]{3,2,1,0:T(8,128)(2,1)}) custom-call(f32[2,512,512]{2,1,0:T(8,128)S(1)} %get-tuple-element.9.refs_0_, f32[2,512,512]{2,1,0:T(8,128)S(1)} %get-tuple-element.10.refs_1_, bf16[2,4,512,512]{3,2,1,0:T(8,128)(2,1)S(1)} %get-tuple-element.11.refs_2_), custom_call_target="tpu_custom_call" | custom-call | tf_op jit(solution)/shard_map/pallas_call | solution.py:420

commit v3 on v2

v3 whole, which is shorter than its diff:
```python
import functools

import jax
import jax.numpy as jnp
from jax import lax
from jax.experimental import pallas as pl
from jax.experimental.pallas import tpu as pltpu
from jax.sharding import PartitionSpec as P


PANEL = 128
STRIP = 16
EIGHT = 8
HALF = 256
ROW_TILE = 16
VMEM = pl.BlockSpec(memory_space=pltpu.VMEM)
HBM = pl.BlockSpec(memory_space=pltpu.HBM)
TN = (((0,), (0,)), ((), ()))


def split(value):
    high = value.astype(jnp.bfloat16)
    low = (value - high.astype(jnp.float32)).astype(jnp.bfloat16)
    return high, low


def product(left, right):
    dot = functools.partial(jnp.dot, preferred_element_type=jnp.float32)
    (lh, ll), (rh, rl) = left, right
    return dot(lh, rh) + (dot(lh, rl) + dot(ll, rh))


def factor_diagonal(work, count):
    lane = lax.broadcasted_iota(jnp.int32, (EIGHT, PANEL), 1)
    sub = lax.broadcasted_iota(jnp.int32, (EIGHT, PANEL), 0)
    lane_tall = lax.broadcasted_iota(jnp.int32, (STRIP, PANEL), 1)
    groups = STRIP // EIGHT

    def spread(value, k):
        return jnp.broadcast_to(value[k : k + 1], value.shape)

    def strip(b, carry):
        start = pl.multiple_of(b * STRIP, STRIP)
        rows = [
            [
                [
                    work[m, pl.ds(pl.multiple_of(start + g * EIGHT, EIGHT), EIGHT), tile_rows(w)]
                    for w in range(2)
                ]
                for g in range(groups)
            ]
            for m in range(count)
        ]
        columns = [
            [
                [
                    jnp.take_along_axis(rows[m][g][0], jnp.full_like(lane, start + c), axis=1)
                    if g >= c // EIGHT
                    else None
                    for g in range(groups)
                ]
                for c in range(STRIP)
            ]
            for m in range(count)
        ]
        roots = [[jnp.zeros((EIGHT, PANEL), jnp.float32)] * groups for _ in range(count)]
        for j in range(STRIP):
            top, at = j // EIGHT, j % EIGHT
            for m in range(count):
                column = columns[m][j]
                root = lax.rsqrt(spread(column[top], at))
                square = root * root
                scaled = [None if v is None else v * square for v in column]
                for c in range(j + 1, STRIP):
                    across = spread(column[c // EIGHT], c % EIGHT)
                    for g in range(c // EIGHT, groups):
                        if c == j + 1:
                            term = (column[g] * across) * square
                        else:
                            term = scaled[g] * across
                        columns[m][c][g] = columns[m][c][g] - term
                roots[m][top] = jnp.where(sub == at, root, roots[m][top])
                line = [spread(v, at) for v in rows[m][top]]
                for g in range(top, groups):
                    below = scaled[g] if g > top else jnp.where(sub > at, scaled[g], 0.0)
                    rows[m][g] = [v - below * x for v, x in zip(rows[m][g], line)]
        for m in range(count):
            final = [
                jnp.concatenate([rows[m][g][w] * roots[m][g] for g in range(groups)], 0)
                for w in range(2)
            ]
            for w in range(2):
                work[m, pl.ds(start, STRIP), tile_rows(w)] = final[w]
            high = [v.astype(jnp.bfloat16).astype(jnp.float32) for v in final]
            low = [v - h for v, h in zip(final, high)]
            after = lane_tall >= start + STRIP
            left_high = jnp.where(after, high[0], 0.0)
            left_low = jnp.where(after, low[0], 0.0)
            left = jnp.concatenate([left_high, left_high, left_low, left_low], 0)
            wide_high, wide_low = jnp.concatenate(high, 1), jnp.concatenate(low, 1)
            right = jnp.concatenate([wide_high, wide_low, wide_high, wide_low], 0)
            work[m] = work[m] - lax.dot_general(
                left.astype(jnp.bfloat16).T,
                right.astype(jnp.bfloat16),
                (((1,), (0,)), ((), ())),
                preferred_element_type=jnp.float32,
            )
        return carry

    lax.fori_loop(0, PANEL // STRIP, strip, 0)


def triangle(order):
    return [(p, q) for p in range(order // PANEL) for q in range(p + 1)]


def factor_reds(blocks, factor, inverse, work, packed):
    count, order = blocks.shape[0], blocks.shape[2]
    row = lax.broadcasted_iota(jnp.int32, (PANEL, PANEL), 0)
    col = lax.broadcasted_iota(jnp.int32, (PANEL, PANEL), 1)
    eye = jnp.where(row == col, 1.0, 0.0).astype(jnp.float32)
    inverse[...] = jnp.zeros_like(inverse)
    factor[...] = jnp.zeros_like(factor)
    for start in range(0, order, PANEL):
        stop = start + PANEL
        here = slice(start, stop)
        for m in range(count):
            work[m, :, :PANEL] = blocks[m, here, here]
            work[m, :, PANEL:] = eye
        factor_diagonal(work, count)
        for m in range(count):
            upper = jnp.where(col >= row, work[m, :, :PANEL], 0.0)
            factor[m, here, here] = upper.T
            small = jnp.where(col <= row, work[m, :, PANEL:], 0.0)
            small_parts = split(small)
            if start:
                inverse[m, here, :start] = product(small_parts, split(inverse[m, here, :start]))
            inverse[m, here, here] = small
            if stop < order:
                across = product(small_parts, split(blocks[m, here, stop:]))
                down = across.T
                factor[m, stop:, here] = down
                down_parts = split(down)
                blocks[m, stop:, stop:] -= product(down_parts, split(across))
                inverse[m, stop:, :stop] -= product(down_parts, split(inverse[m, here, :stop]))
    for m in range(count):
        for n, (p, q) in enumerate(triangle(order)):
            tile = inverse[m, p * PANEL : (p + 1) * PANEL, q * PANEL : (q + 1) * PANEL]
            packed[m, 0, n], packed[m, 1, n] = split(tile)


def triangle_index(p, q):
    return p * (p + 1) // 2 + q


def off_diagonal(order):
    return [(p, q) for p, q in triangle(order) if p != q]


def grid_of_panel():
    row = lax.broadcasted_iota(jnp.int32, (PANEL, PANEL), 0)
    col = lax.broadcasted_iota(jnp.int32, (PANEL, PANEL), 1)
    return row, col


def compact_rows(order):
    panels = order // PANEL
    return (len(off_diagonal(order)) + panels // 2) * PANEL + ROW_TILE


def tile_rows(n):
    return slice(n * PANEL, (n + 1) * PANEL)


def compact(tile_of, order, out, flip):
    row, col = grid_of_panel()
    pairs = off_diagonal(order)
    for n, (p, q) in enumerate(pairs):
        out[tile_rows(n), :] = tile_of(p, q).astype(jnp.bfloat16)
    lines = []
    for k in range(0, order // PANEL, 2):
        first, second = tile_of(k, k), tile_of(k + 1, k + 1)
        other = second.T if flip else second
        joined = jnp.where(row >= col, first, other)
        out[tile_rows(len(pairs) + k // 2), :] = joined.astype(jnp.bfloat16)
        lines.append(jnp.sum(jnp.where(row == col, second, 0.0), axis=0, keepdims=True))
    lines.append(jnp.zeros((ROW_TILE - len(lines), PANEL), jnp.float32))
    base = compact_rows(order) - ROW_TILE
    out[base:, :] = jnp.concatenate(lines, 0).astype(jnp.bfloat16)


def spread_diagonal(packed, order, symmetric):
    row, col = grid_of_panel()
    skip = len(off_diagonal(order))
    base = compact_rows(order) - ROW_TILE
    lines = packed[base:, :].astype(jnp.float32)
    tiles = []
    for k in range(order // PANEL // 2):
        joined = packed[tile_rows(skip + k), :].astype(jnp.float32)
        turned = joined.T
        line = jnp.broadcast_to(lines[k : k + 1, :], joined.shape)
        tiles.append(jnp.where(row >= col, joined, turned if symmetric else 0.0))
        upper = joined if symmetric else 0.0
        tiles.append(jnp.where(row == col, line, jnp.where(col < row, turned, upper)))
    return tiles


def solve(parts, coupling, flipped, out):
    order = out.shape[0]
    axes = (((1,), (1 if flipped else 0,)), ((), ()))
    zero = jnp.zeros((PANEL, PANEL), jnp.bfloat16)
    for top in range(0, order // PANEL, 2):
        stop = (top + 2) * PANEL
        right = coupling[:, :stop] if flipped else coupling[:stop, :]
        value = None
        for tile_of in parts:
            lines = [
                jnp.concatenate([tile_of(p, q) if q <= p else zero for q in range(top + 2)], 1)
                for p in (top, top + 1)
            ]
            left = jnp.concatenate(lines, 0)
            term = lax.dot_general(left, right, axes, preferred_element_type=jnp.float32)
            value = term if value is None else value + term
        out[top * PANEL : stop, :] = value.astype(jnp.bfloat16)


def own_parts(packed, m):
    return [
        lambda p, q, part=part: packed[m, part, triangle_index(p, q)] for part in range(2)
    ]


def far_parts(packed, diagonal, order):
    for k, tile in enumerate(spread_diagonal(packed, order, False)):
        diagonal[k] = tile.astype(jnp.bfloat16)
    place = {pair: n for n, pair in enumerate(off_diagonal(order))}
    return [lambda p, q: diagonal[p] if p == q else packed[tile_rows(place[p, q]), :]]


def grams(order, terms):
    def body(step, carry):
        rows = pl.ds(pl.multiple_of(step * HALF, HALF), HALF)
        for pairs, emit in terms:
            total = None
            for left, right in pairs:
                value = lax.dot_general(
                    left[:, rows], right[...], TN, preferred_element_type=jnp.float32
                )
                total = value if total is None else total + value
            emit(rows, total)
        return carry

    lax.fori_loop(0, order // HALF, body, 0)


def compact_gram(solved, out):
    order = solved.shape[0]
    strips = [
        lax.dot_general(
            solved[:, tile_rows(p)],
            solved[:, : (p + 1) * PANEL],
            TN,
            preferred_element_type=jnp.float32,
        )
        for p in range(order // PANEL)
    ]
    compact(lambda p, q: strips[p][:, tile_rows(q)], order, out, False)


def difference_into(start, out):
    def emit(rows, total):
        out[rows, :] = start[rows, :] - total

    return emit


def negate_into(out):
    def emit(rows, total):
        out[rows, :] = (-total).astype(jnp.bfloat16)

    return emit


def negate_with(extra, out):
    def emit(rows, total):
        out[rows, :] = (-(total + extra[rows, :].astype(jnp.float32))).astype(jnp.bfloat16)

    return emit


def plain_into(out):
    def emit(rows, total):
        out[rows, :] = total.astype(jnp.bfloat16)

    return emit


class Mover:
    def __init__(self, sems):
        self.sems, self.copies = sems, []

    def start(self, src, dst):
        copy = pltpu.make_async_copy(src, dst, self.sems.at[len(self.copies)])
        copy.start()
        self.copies.append([copy, False])
        return len(self.copies) - 1

    def wait(self, *which):
        for k in which or range(len(self.copies)):
            copy, done = self.copies[k]
            if not done:
                copy.wait()
                self.copies[k][1] = True


def factor_kernel(
    diag, hor, ver,
    factor_out, packed, mine, down, give_down, flat, upright, start,
    blocks, factor, inverse, work, sems,
):
    order = blocks.shape[1]
    mover = Mover(sems)
    for m in range(2):
        mover.start(diag.at[m, m], blocks.at[m])
    mover.wait()
    mover.start(ver, upright)
    mover.start(hor, flat)
    mover.start(diag.at[0, 1], start.at[0])
    mover.start(diag.at[1, 0], start.at[1])
    factor_reds(blocks, factor, inverse, work, packed)
    out = mover.start(factor, factor_out)
    compact(lambda p, q: inverse[0, tile_rows(p), tile_rows(q)], order, mine, True)
    mover.wait(*range(2, out))
    solve(own_parts(packed, 1), upright.at[1, 1], False, down)
    compact_gram(down, give_down)
    mover.wait(out)


def give_kernel(packed, down, flat, right, give_sym, give_cross):
    order = right.shape[0]
    solve(own_parts(packed, 1), flat.at[1, 1], False, right)
    compact_gram(right, give_sym)
    grams(order, [([(right, down)], plain_into(give_cross))])


def own_kernel(
    packed, down_, right_, start, flat, upright,
    schur0, schur1, up_, left_, made,
    own,
):
    order = up_.shape[0]
    one, zero = own_parts(packed, 1), own_parts(packed, 0)
    down, across = own.at[0], own.at[1]
    solve(one, flat.at[1, 0], True, left_)
    solve(one, upright.at[0, 1], True, up_)
    solve(zero, upright.at[0, 0], False, down)
    solve(zero, flat.at[0, 0], False, across)
    grams(
        order,
        [
            ([(across, across), (up_, up_)], difference_into(start.at[0], schur0)),
            ([(down, down), (left_, left_)], difference_into(start.at[1], schur1)),
            ([(up_, down_)], negate_into(made.at[0])),
            ([(across, down), (up_, left_)], negate_into(made.at[1])),
            ([(left_, right_)], negate_into(made.at[2])),
        ],
    )


def right_kernel(
    inv, far_down, far_right, flat, schur_in, up_, right_, ready,
    schur, made, links_out,
    diagonal, near, sems,
):
    order = up_.shape[0]
    mover = Mover(sems)
    mover.start(ready.at[0], links_out.at[0, 0, 1])
    mover.start(ready.at[1], links_out.at[0, 0, 3])
    mover.start(ready.at[2], links_out.at[1, 0, 0])
    far = far_parts(inv, diagonal, order)
    near_left, near_down, near_right = near.at[0], near.at[1], near.at[2]
    solve(far, flat.at[0, 1], True, near_left)
    solve(far, far_down, False, near_down)
    solve(far, far_right, False, near_right)
    grams(
        order,
        [
            ([(near_left, near_left)], difference_into(schur_in, schur)),
            ([(near_left, near_right)], negate_into(made.at[0])),
            ([(up_, right_), (near_left, near_down)], negate_into(made.at[1])),
        ],
    )
    mover.wait()


def below_kernel(
    inv, far_down, far_right, far_left, upright, schur_in, down_, left_, got_cross,
    ready, links_in,
    schur, links_out,
    diagonal, near, made, sems,
):
    order = down_.shape[0]
    mover = Mover(sems)
    mover.start(ready.at[0], links_out.at[0, 0, 0])
    mover.start(ready.at[1], links_out.at[0, 0, 2])
    far = far_parts(inv, diagonal, order)
    below_up, below_left, below_down, below_right = (near.at[k] for k in range(4))
    solve(far, upright.at[1, 0], True, below_up)
    solve(far, far_down, False, below_down)
    solve(far, far_right, False, below_right)
    solve(far, far_left, True, below_left)
    grams(
        order,
        [
            ([(below_up, below_up)], difference_into(schur_in, schur)),
            ([(below_up, below_down)], negate_into(made.at[0])),
            ([(left_, down_), (below_up, below_right)], negate_into(made.at[1])),
        ],
    )
    mover.start(made.at[0], links_out.at[1, 0, 1])
    mover.start(made.at[1], links_out.at[1, 0, 2])
    grams(order, [([(below_up, below_left)], negate_with(got_cross, made.at[2]))])
    mover.start(made.at[2], links_out.at[1, 0, 3])
    mover.wait()


def subtracted(packed, whole, out, mover, place):
    order = out.shape[0]
    panels = order // PANEL
    spread = spread_diagonal(packed, order, True)
    index = {pair: n for n, pair in enumerate(off_diagonal(order))}
    tiles = {pair: packed[tile_rows(n), :].astype(jnp.float32) for pair, n in index.items()}
    for p in range(panels):
        line = [
            spread[p] if q == p else tiles[p, q] if q < p else tiles[q, p].T
            for q in range(panels)
        ]
        out[tile_rows(p), :] = whole[tile_rows(p), :] - jnp.concatenate(line, 1)
        mover.start(out.at[tile_rows(p)], place.at[tile_rows(p)])


def schur_odd_kernel(partial, got, schur_out, schur, sems):
    mover = Mover(sems)
    subtracted(got, partial, schur, mover, schur_out.at[1, 0])
    mover.wait()


def schur_even_kernel(partial, got, schur_in, schur_out, schur, sems):
    mover = Mover(sems)
    subtracted(got, partial, schur, mover, schur_out.at[0, 0])
    mover.wait()


def first_kernel(hor, ver, down, right, left, sems):
    mover = Mover(sems)
    mover.start(ver.at[0, 0], down)
    mover.start(hor.at[0, 0], right)
    mover.start(hor.at[0, 1], left)
    mover.wait()


def called(kernel, ins, outs, scratch, flops, aliases=None):
    size = sum(a.size * a.dtype.itemsize for a, _ in ins)
    held = [
        pltpu.with_memory_space_constraint(a, pltpu.HBM) if spec is HBM else a for a, spec in ins
    ]
    return pl.pallas_call(
        kernel,
        out_shape=tuple(jax.ShapeDtypeStruct(shape, dtype) for shape, dtype, _ in outs),
        in_specs=[spec for _, spec in ins],
        out_specs=tuple(spec for _, _, spec in outs),
        scratch_shapes=scratch,
        input_output_aliases=aliases or {},
        compiler_params=pltpu.CompilerParams(vmem_limit_bytes=24 * 2**20),
        cost_estimate=pl.CostEstimate(flops=flops, bytes_accessed=size, transcendentals=0),
    )(*held)


def shifted(value, down, across):
    rows, cols = lax.axis_size("row"), lax.axis_size("col")
    pairs = [
        (i * cols + j, (i + down) % rows * cols + (j + across) % cols)
        for i in range(rows)
        for j in range(cols)
    ]
    return lax.ppermute(value, ("row", "col"), pairs)


def on_device(diag_blocks, horizontal, vertical):
    order = diag_blocks.shape[-1]
    assert diag_blocks.shape[:2] == (2, 2)
    tiles = len(triangle(order))
    square = (order, order)
    bf16, f32 = jnp.bfloat16, jnp.float32
    dense = (compact_rows(order), PANEL)
    diagonal = pltpu.VMEM((order // PANEL, PANEL, PANEL), bf16)

    def sems(n):
        return pltpu.SemaphoreType.DMA((n,))

    down_first, right_first, left_first = called(
        first_kernel,
        [(horizontal, HBM), (vertical, HBM)],
        [(square, bf16, VMEM)] * 3,
        [sems(3)],
        1_000_000,
    )
    down_up = shifted(down_first, -1, 0)
    right_up = shifted(right_first, -1, 0)
    left_up = shifted(left_first, -1, 1)
    down_right = shifted(down_first, 0, -1)
    right_right = shifted(right_first, 0, -1)
    pairs = (2, 2) + square
    factor, packed, mine, down, give_down, flat, upright, start = called(
        factor_kernel,
        [(diag_blocks, HBM), (horizontal, HBM), (vertical, HBM)],
        [
            ((2,) + square, f32, HBM),
            ((2, 2, tiles, PANEL, PANEL), bf16, VMEM),
            (dense, bf16, VMEM),
            (square, bf16, VMEM),
            (dense, bf16, VMEM),
            (pairs, bf16, VMEM),
            (pairs, bf16, VMEM),
            ((2,) + square, f32, VMEM),
        ],
        [
            pltpu.VMEM((2,) + square, f32),
            pltpu.VMEM((2,) + square, f32),
            pltpu.VMEM((2,) + square, f32),
            pltpu.VMEM((2, PANEL, 2 * PANEL), f32),
            sems(7),
        ],
        20_000_000_000,
    )
    inverse_up = shifted(mine, -1, 0)
    inverse_right = shifted(mine, 0, -1)
    got_above = shifted(give_down, 1, 0)
    right, give_sym, give_cross = called(
        give_kernel,
        [(packed, VMEM), (down, VMEM), (flat, VMEM)],
        [(square, bf16, VMEM), (dense, bf16, VMEM), (square, bf16, VMEM)],
        [],
        1_000_000_000,
    )
    got_sym = shifted(give_sym, 0, 1)
    got_cross = shifted(give_cross, 0, 1)
    links_shape = ((2, 1, 4) + square, bf16, HBM)
    schur0, schur1, up, left, ready = called(
        own_kernel,
        [(packed, VMEM), (down, VMEM), (right, VMEM), (start, VMEM), (flat, VMEM), (upright, VMEM)],
        [
            (square, f32, VMEM), (square, f32, VMEM),
            (square, bf16, VMEM), (square, bf16, VMEM), ((3,) + square, bf16, VMEM),
        ],
        [pltpu.VMEM((2,) + square, bf16)],
        3_000_000_000,
    )
    schur0, ready, links = called(
        right_kernel,
        [
            (inverse_right, VMEM), (down_right, VMEM), (right_right, VMEM), (flat, VMEM),
            (schur0, VMEM), (up, VMEM), (right, VMEM), (ready, VMEM),
        ],
        [(square, f32, VMEM), ((2,) + square, bf16, VMEM), links_shape],
        [diagonal, pltpu.VMEM((3,) + square, bf16), sems(3)],
        2_000_000_000,
    )
    schur1, links = called(
        below_kernel,
        [
            (inverse_up, VMEM), (down_up, VMEM), (right_up, VMEM), (left_up, VMEM),
            (upright, VMEM), (schur1, VMEM), (down, VMEM), (left, VMEM),
            (got_cross, VMEM), (ready, VMEM), (links, HBM),
        ],
        [(square, f32, VMEM), links_shape],
        [
            diagonal, pltpu.VMEM((4,) + square, bf16), pltpu.VMEM((3,) + square, bf16), sems(5),
        ],
        3_000_000_000,
        {10: 1},
    )
    schur_shape = ((2, 1) + square, f32, HBM)
    strips = sems(order // PANEL)
    (schur,) = called(
        schur_odd_kernel,
        [(schur1, VMEM), (got_sym, VMEM)],
        [schur_shape],
        [pltpu.VMEM(square, f32), strips],
        300_000_000,
    )
    (schur,) = called(
        schur_even_kernel,
        [(schur0, VMEM), (got_above, VMEM), (schur, HBM)],
        [schur_shape],
        [pltpu.VMEM(square, f32), strips],
        300_000_000,
        {2: 0},
    )
    return (factor[:, None], schur, links)


def solution(mesh):
    in_specs = (
        P("row", "col", None, None),
        P("row", "col", None, None),
        P("row", "col", None, None),
    )
    out_specs = (
        P("row", "col", None, None),
        P("row", "col", None, None),
        P("row", "col", None, None, None),
    )
    return jax.shard_map(
        on_device, mesh=mesh, in_specs=in_specs, out_specs=out_specs, check_vma=False
    )
```

time: 57.5 us -> 84.5 us (1.47)
  waiting for transfers between devices: 0 us -> 31.8 us
  Pallas kernels: 56.7 us -> 39.1 us
  starting transfers between devices: 0 us -> 12.7 us
    ppermute x0 -> x10, waiting for transfers between devices: none -> 31.8 us  [shifted(): return lax.ppermute(value, ('row', 'col'), pairs)]
    pallas_call x2 -> x8, Pallas kernels: 56.7 us -> 39.1 us  [called(): pl.pallas_call(kernel, out_shape=tuple((jax.ShapeDtypeStruct(shape, dtype...]
    ppermute x0 -> x10, starting transfers between devices: none -> 12.7 us  [shifted(): return lax.ppermute(value, ('row', 'col'), pairs)]
  transfers between devices with their start and end apart: 0 -> 10, of which waited for: 0 -> 3; matrix products, arithmetic and copies ran while one was open for 0% -> 0% of each run, Pallas kernels for 0% -> 43%
where the time goes in v3:
time: 84.5 us; the launch traced here: 84.3 us
  Pallas kernels  39.1 us (46%)
  waiting for transfers between devices  31.8 us (38%)
  starting transfers between devices  12.7 us (15%)
    pallas_call x8, Pallas kernels, called(): pl.pallas_call(kernel, out_shape=tuple((jax.ShapeDtypeStruct(shape, dtype...  39.1 us
    ppermute x10, waiting for transfers between devices, shifted(): return lax.ppermute(value, ('row', 'col'), pairs)  31.8 us
    ppermute x10, starting transfers between devices, shifted(): return lax.ppermute(value, ('row', 'col'), pairs)  12.7 us
  transfers between devices with their start and end apart: 10, of which 3 were waited for; matrix products, arithmetic and copies ran while one was open for 0% of the time, Pallas kernels for 43%

profile of v3, /device:TPU:0, one launch (start us, length us, event | category | flops | bytes accessed | tf_op | source)
XLA Modules:
  0.0 84.3 jit_solution(5824784151954405703)
XLA Ops:
  0.6 1.4 %shard_map.59 = (bf16[512,512]{1,0:T(8,128)(2,1)S(1)}, bf16[512,512]{1,0:T(8,128)(2,1)S(1)}, bf16[512,512]{1,0:T(8,128)(2,1)S(1)}) custom-call(bf16[2,2,512,512]{3,2,1,0:T(8,128)(2,1)} %hor.3, bf16[2,2,512,512]{3,2,1,0:T(8,128)(2,1)} %ver.3), custom_call_target="tpu_custom_call" | custom-call | flops 1000000 | bytes 4194304 | tf_op jit(solution)/shard_map/pallas_call | solution.py:467
  2.0 3.4 %collective-permute-start.1 = (bf16[512,512]{1,0:T(8,128)(2,1)S(1)}, bf16[512,512]{1,0:T(8,128)(2,1)S(1)}, u32[]{:S(2)}, u32[]{:S(2)}) collective-permute-start(bf16[512,512]{1,0:T(8,128)(2,1)S(1)} %get-tuple-element.29), channel_id=1, source_target_pairs={{0,7},{1,0},{2,1},{3,2},{4,3},{5,4},{6,5},{7,6},{8,15},{9,8},{10,9... | collective-permute-start | bytes 1572872 | tf_op jit(solution)/shard_map/ppermute | solution.py:486
  5.4 0.7 collective-permute-start.2
  6.1 22.9 %shard_map.58 = (f32[2,512,512]{2,1,0:T(8,128)}, bf16[2,2,10,128,128]{4,3,2,1,0:T(8,128)(2,1)S(1)}, bf16[1040,128]{1,0:T(8,128)(2,1)S(1)}, bf16[512,512]{1,0:T(8...) custom-call(f32[2,2,512,512]{3,2,1,0:T(8,128)} %diag.1, ...), custom_call_target="tpu_custom_call" | custom-call | flops 20000000000 | bytes 8388608 | tf_op jit(solution)/shard_map/pallas_call | solution.py:467
  29.0 0.1 collective-permute-start
  29.2 3.6 %collective-permute-start.5 = (bf16[512,512]{1,0:T(8,128)(2,1)S(1)}, bf16[512,512]{1,0:T(8,128)(2,1)S(1)}, u32[]{:S(2)}, u32[]{:S(2)}) collective-permute-start(bf16[512,512]{1,0:T(8,128)(2,1)S(1)} %get-tuple-element.29), channel_id=1, source_target_pairs={{0,24},{1,25},{2,26},{3,27},{4,28},{5,29},{6,30},{7,31},{8,0},{9,1... | collective-permute-start | bytes 1572872 | tf_op jit(solution)/shard_map/ppermute | solution.py:486
  32.7 0.2 collective-permute-start.7
  33.0 1.7 %shard_map.60 = (bf16[512,512]{1,0:T(8,128)(2,1)S(1)}, bf16[1040,128]{1,0:T(8,128)(2,1)S(1)}, bf16[512,512]{1,0:T(8,128)(2,1)S(1)}) custom-call(bf16[2,2,10,128,128]{4,3,2,1,0:T(8,128)(2,1)S(1)} %get-tuple-element.32.packed, bf16[512,512]{1,0:T(8,128)(2,1)S(1)} %get-tuple-element.33.down.down_, bf16[2,2,512,512]{3,2,1,0:T(8,128)(2,1)S(1)} %get-tuple-element.31.flat), custom_call_target="tpu_custom_call" | custom-call | flops 1000000000 | bytes 3932160 | tf_op jit(solution)/shard_map/pallas_call | solution.py:467
  34.7 0.0 collective-permute-done.inv
  34.7 2.0 %collective-permute-start.6 = (bf16[512,512]{1,0:T(8,128)(2,1)S(1)}, bf16[512,512]{1,0:T(8,128)(2,1)S(1)}, u32[]{:S(2)}, u32[]{:S(2)}) collective-permute-start(bf16[512,512]{1,0:T(8,128)(2,1)S(1)} %get-tuple-element.30), channel_id=1, source_target_pairs={{0,24},{1,25},{2,26},{3,27},{4,28},{5,29},{6,30},{7,31},{8,0},{9,1... | collective-permute-start | bytes 1572872 | tf_op jit(solution)/shard_map/ppermute | solution.py:486
  36.7 1.7 %collective-permute-start.8 = (bf16[512,512]{1,0:T(8,128)(2,1)S(1)}, bf16[512,512]{1,0:T(8,128)(2,1)S(1)}, u32[]{:S(2)}, u32[]{:S(2)}) collective-permute-start(bf16[512,512]{1,0:T(8,128)(2,1)S(1)} %get-tuple-element.45), channel_id=1, source_target_pairs={{0,1},{1,2},{2,3},{3,4},{4,5},{5,6},{6,7},{7,0},{8,9},{9,10},{10,1... | collective-permute-start | bytes 1572872 | tf_op jit(solution)/shard_map/ppermute | solution.py:486
  38.4 0.0 collective-permute-done.2.far_right
  38.4 0.4 collective-permute-start.4
  38.8 4.4 %shard_map.61 = (f32[512,512]{1,0:T(8,128)S(1)}, f32[512,512]{1,0:T(8,128)S(1)}, bf16[512,512]{1,0:T(8,128)(2,1)S(1)}, bf16[512,512]{1,0:T(8,128)(2,1)S(1)}, bf16[3,512,512]{2,1,0:T(8,128)(2,1)S(1)}) custom-call(bf16[2,2,10,128,128]{4,3,2,1,0:T(8,128)(2,1)S(1)} %get-tuple-element.32.packed, bf16[512,512]{1,0:T(8,128)(2,1)S(1)} %get-tuple-element.33.down.down_, ...), custom_call_target="tpu_custom_call" | custom-call | flops 3000000000 | bytes 8650752 | tf_op jit(solution)/shard_map/pallas_call | solution.py:467
  43.3 2.4 %shard_map.62 = (f32[512,512]{1,0:T(8,128)S(1)}, bf16[2,512,512]{2,1,0:T(8,128)(2,1)S(1)}, bf16[2,1,4,512,512]{4,3,2,1,0:T(8,128)(2,1)}) custom-call(bf16[1040,128]{1,0:T(8,128)(2,1)S(1)} %collective-permute-done.inv, bf16[512,512]{1,0:T(8,128)(2,1)S(1)} %collective-permute-done.1.far_down, bf16[512,512]{1,0:T(8,128)(2,1)S(1)} %collective-permute-done.2.far_right, ...), custom_call_target="tpu_custom_call" | custom-call | flops 2000000000 | bytes 7081984 | tf_op jit(solution)/shard_map/pallas_call | solution.py:467
  45.6 27.1 %collective-permute-done.4.inv = bf16[1040,128]{1,0:T(8,128)(2,1)S(1)} collective-permute-done((bf16[1040,128]{1,0:T(8,128)(2,1)S(1)}, bf16[1040,128]{1,0:T(8,128)(2,1)S(1)}, u32[]{:S(2)}, u32[]{:S(2)}) %collective-permute-start.4) | collective-permute-done | bytes 266272 | tf_op jit(solution)/shard_map/ppermute | solution.py:486
  72.7 0.5 collective-permute-start.3
  73.2 0.0 collective-permute-done.7.far_left
  73.2 0.0 collective-permute-done.6.far_right
  73.2 4.0 %shard_map.63 = (f32[512,512]{1,0:T(8,128)S(1)}, bf16[2,1,4,512,512]{4,3,2,1,0:T(8,128)(2,1)}) custom-call(bf16[1040,128]{1,0:T(8,128)(2,1)S(1)} %collective-permute-done.4.inv, bf16[512,512]{1,0:T(8,128)(2,1)S(1)} %collective-permute-done.5.far_down, bf16[512,512]{1,0:T(8,128)(2,1)S(1)} %collective-permute-done.6.far_right, ...), custom_call_target="tpu_custom_call", output_to_operand_aliasing={{1}: (10, {})} | custom-call | flops 3000000000 | bytes 11800576 | tf_op jit(solution)/shard_map/pallas_call | solution.py:467
  77.3 2.7 %collective-permute-done.9.got = bf16[1040,128]{1,0:T(8,128)(2,1)S(1)} collective-permute-done((bf16[1040,128]{1,0:T(8,128)(2,1)S(1)}, bf16[1040,128]{1,0:T(8,128)(2,1)S(1)}, u32[]{:S(2)}, u32[]{:S(2)}) %collective-permute-start.9) | collective-permute-done | bytes 266272 | tf_op jit(solution)/shard_map/ppermute | solution.py:486
  79.9 1.2 %shard_map.64.schur_in = f32[2,1,512,512]{3,2,1,0:T(8,128)} custom-call(f32[512,512]{1,0:T(8,128)S(1)} %get-tuple-element.48.partial, bf16[1040,128]{1,0:T(8,128)(2,1)S(1)} %collective-permute-done.9.got), custom_call_target="tpu_custom_call" | custom-call | flops 300000000 | bytes 1314816 | tf_op jit(solution)/shard_map/pallas_call | solution.py:467
  81.1 2.0 %collective-permute-done.3.got = bf16[1040,128]{1,0:T(8,128)(2,1)S(1)} collective-permute-done((bf16[1040,128]{1,0:T(8,128)(2,1)S(1)}, bf16[1040,128]{1,0:T(8,128)(2,1)S(1)}, u32[]{:S(2)}, u32[]{:S(2)}) %collective-permute-start.3) | collective-permute-done | bytes 266272 | tf_op jit(solution)/shard_map/ppermute | solution.py:486
  83.1 1.2 %shard_map.65 = f32[2,1,512,512]{3,2,1,0:T(8,128)} custom-call(f32[512,512]{1,0:T(8,128)S(1)} %get-tuple-element.40.partial, bf16[1040,128]{1,0:T(8,128)(2,1)S(1)} %collective-permute-done.3.got, f32[2,1,512,512]{3,2,1,0:T(8,128)} %shard_map.64.schur_in), custom_call_target="tpu_custom_call", output_to_operand_aliasing={{}: (2, {})} | custom-call | flops 300000000 | bytes 3411968 | tf_op jit(solution)/shard_map/pallas_call | solution.py:467
  (4 shorter events, 0.0 us)
Async XLA Ops:
  2.0 34.7 %collective-permute-start.1 = (bf16[512,512]{1,0:T(8,128)(2,1)S(1)}, bf16[512,512]{1,0:T(8,128)(2,1)S(1)}, u32[]{:S(2)}, u32[]{:S(2)}) collective-permute-start(bf16[512,512]{1,0:T(8,128)(2,1)S(1)} %get-tuple-element.29), channel_id=1, source_target_pairs={{0,7},{1,0},{2,1},{3,2},{4,3},{5,4},{6,5},{7,6},{8,15},{9,8},{10,9... | collective-permute-start | bytes 1572872 | tf_op jit(solution)/shard_map/ppermute | solution.py:486
  5.4 32.9 %collective-permute-start.2 = (bf16[512,512]{1,0:T(8,128)(2,1)S(1)}, bf16[512,512]{1,0:T(8,128)(2,1)S(1)}, u32[]{:S(2)}, u32[]{:S(2)}) collective-permute-start(bf16[512,512]{1,0:T(8,128)(2,1)S(1)} %get-tuple-element.30), channel_id=1, source_target_pairs={{0,7},{1,0},{2,1},{3,2},{4,3},{5,4},{6,5},{7,6},{8,15},{9,8},{10,9... | collective-permute-start | bytes 1572872 | tf_op jit(solution)/shard_map/ppermute | solution.py:486
  29.0 5.6 %collective-permute-start = (bf16[1040,128]{1,0:T(8,128)(2,1)S(1)}, bf16[1040,128]{1,0:T(8,128)(2,1)S(1)}, u32[]{:S(2)}, u32[]{:S(2)}) collective-permute-start(bf16[1040,128]{1,0:T(8,128)(2,1)S(1)} %get-tuple-element.28), channel_id=1, source_target_pairs={{0,7},{1,0},{2,1},{3,2},{4,3},{5,4},{6,5},{7,6},{8,15},{9,8},{10,9... | collective-permute-start | bytes 798728 | tf_op jit(solution)/shard_map/ppermute | solution.py:486
  29.2 44.0 %collective-permute-start.5 = (bf16[512,512]{1,0:T(8,128)(2,1)S(1)}, bf16[512,512]{1,0:T(8,128)(2,1)S(1)}, u32[]{:S(2)}, u32[]{:S(2)}) collective-permute-start(bf16[512,512]{1,0:T(8,128)(2,1)S(1)} %get-tuple-element.29), channel_id=1, source_target_pairs={{0,24},{1,25},{2,26},{3,27},{4,28},{5,29},{6,30},{7,31},{8,0},{9,1... | collective-permute-start | bytes 1572872 | tf_op jit(solution)/shard_map/ppermute | solution.py:486
  32.7 40.5 %collective-permute-start.7 = (bf16[512,512]{1,0:T(8,128)(2,1)S(1)}, bf16[512,512]{1,0:T(8,128)(2,1)S(1)}, u32[]{:S(2)}, u32[]{:S(2)}) collective-permute-start(bf16[512,512]{1,0:T(8,128)(2,1)S(1)} %get-tuple-element.42), channel_id=1, source_target_pairs={{0,25},{1,26},{2,27},{3,28},{4,29},{5,30},{6,31},{7,24},{8,1},{9,2... | collective-permute-start | bytes 1572872 | tf_op jit(solution)/shard_map/ppermute | solution.py:486
  34.7 38.5 %collective-permute-start.6 = (bf16[512,512]{1,0:T(8,128)(2,1)S(1)}, bf16[512,512]{1,0:T(8,128)(2,1)S(1)}, u32[]{:S(2)}, u32[]{:S(2)}) collective-permute-start(bf16[512,512]{1,0:T(8,128)(2,1)S(1)} %get-tuple-element.30), channel_id=1, source_target_pairs={{0,24},{1,25},{2,26},{3,27},{4,28},{5,29},{6,30},{7,31},{8,0},{9,1... | collective-permute-start | bytes 1572872 | tf_op jit(solution)/shard_map/ppermute | solution.py:486
  36.7 36.5 %collective-permute-start.8 = (bf16[512,512]{1,0:T(8,128)(2,1)S(1)}, bf16[512,512]{1,0:T(8,128)(2,1)S(1)}, u32[]{:S(2)}, u32[]{:S(2)}) collective-permute-start(bf16[512,512]{1,0:T(8,128)(2,1)S(1)} %get-tuple-element.45), channel_id=1, source_target_pairs={{0,1},{1,2},{2,3},{3,4},{4,5},{5,6},{6,7},{7,0},{8,9},{9,10},{10,1... | collective-permute-start | bytes 1572872 | tf_op jit(solution)/shard_map/ppermute | solution.py:486
  38.4 34.3 %collective-permute-start.4 = (bf16[1040,128]{1,0:T(8,128)(2,1)S(1)}, bf16[1040,128]{1,0:T(8,128)(2,1)S(1)}, u32[]{:S(2)}, u32[]{:S(2)}) collective-permute-start(bf16[1040,128]{1,0:T(8,128)(2,1)S(1)} %get-tuple-element.28), channel_id=1, source_target_pairs={{0,24},{1,25},{2,26},{3,27},{4,28},{5,29},{6,30},{7,31},{8,0},{9,1... | collective-permute-start | bytes 798728 | tf_op jit(solution)/shard_map/ppermute | solution.py:486
  72.7 10.4 %collective-permute-start.3 = (bf16[1040,128]{1,0:T(8,128)(2,1)S(1)}, bf16[1040,128]{1,0:T(8,128)(2,1)S(1)}, u32[]{:S(2)}, u32[]{:S(2)}) collective-permute-start(bf16[1040,128]{1,0:T(8,128)(2,1)S(1)} %get-tuple-element.41), channel_id=1, source_target_pairs={{0,8},{1,9},{2,10},{3,11},{4,12},{5,13},{6,14},{7,15},{8,16},{9,17... | collective-permute-start | bytes 798728 | tf_op jit(solution)/shard_map/ppermute | solution.py:486
  73.2 6.7 %collective-permute-start.9 = (bf16[1040,128]{1,0:T(8,128)(2,1)S(1)}, bf16[1040,128]{1,0:T(8,128)(2,1)S(1)}, u32[]{:S(2)}, u32[]{:S(2)}) collective-permute-start(bf16[1040,128]{1,0:T(8,128)(2,1)S(1)} %get-tuple-element.49), channel_id=1, source_target_pairs={{0,1},{1,2},{2,3},{3,4},{4,5},{5,6},{6,7},{7,0},{8,9},{9,10},{10,1... | collective-permute-start | bytes 798728 | tf_op jit(solution)/shard_map/ppermute | solution.py:486
